TPU v7x, 32 devices: a whole 2x2x4 slice. The times are simulated.
32 devices in a mesh: dp: 2 (over x), tp: 4 (over z), sp: 4 (over y, core).
Axes of the slice: x: 2, y: 2, z: 4, core: 2. Of those that a mesh axis runs over, the one named last changes fastest.
Arguments:
- hidden: bfloat16 [4, 128, 2560], P(None, 'dp'), parts along dimension 1
- start_pos: int32 [128], P('dp'), parts along dimension 0
- k_cache: bfloat16 [128, 1024, 8, 128], P('dp', 'sp', 'tp'), parts along dimension 0
- v_cache: bfloat16 [128, 1024, 8, 128], P('dp', 'sp', 'tp'), parts along dimension 0
- w_q: bfloat16 [2560, 4096], P(None, 'tp')
- w_k: bfloat16 [2560, 1024], P(None, 'tp')
- w_v: bfloat16 [2560, 1024], P(None, 'tp')
- w_o: bfloat16 [4096, 2560], P('tp')
- w_gate: bfloat16 [2560, 9728], P(None, 'tp')
- w_up: bfloat16 [2560, 9728], P(None, 'tp')
- w_down: bfloat16 [9728, 2560], P('tp')
- attn_norm: bfloat16 [2560], replicated
- mlp_norm: bfloat16 [2560], replicated
- q_gain: bfloat16 [128], replicated
- k_gain: bfloat16 [128], replicated
Outputs:
- output 1: bfloat16 [4, 128, 2560], P(None, 'dp'), parts along dimension 1
- output 2: bfloat16 [128, 1024, 8, 128], P('dp', 'sp', 'tp'), parts along dimension 0
- output 3: bfloat16 [128, 1024, 8, 128], P('dp', 'sp', 'tp'), parts along dimension 0
There are 2 independent parts. A program takes and returns all parts, laid end to end along the dimension named above; an argument that names none is the same for every part.
All inputs are finite; a program needn't handle non-finite values.
Results may differ from a plain program's by a relative error of at most 0.00859188.
Values sent between devices are 32-bit elements.
A program may use at most 1 GiB of HBM per device.

v0:
```python
import jax
import jax.numpy as jnp
from jax import lax
from jax.sharding import PartitionSpec as P

ROPE_BASE = 1000000.0
NORM_EPS = 1e-06
NEG_BIG = -1e30


def rms_scale(values, gain_vec):
    wide_vals = values.astype(jnp.float32)
    inv_rms = lax.rsqrt(jnp.mean(wide_vals * wide_vals, axis=-1, keepdims=True) + NORM_EPS)
    return wide_vals * inv_rms * gain_vec.astype(jnp.float32)


def apply_rope(vector, tok_pos):
    head_dim = vector.shape[-1]
    half_dim = head_dim // 2
    freqs = ROPE_BASE ** (-(jnp.arange(half_dim, dtype=jnp.float32) * (2.0 / head_dim)))
    angles = tok_pos.astype(jnp.float32)[:, None] * freqs[None, :]
    cos_tab = jnp.cos(angles)[:, None, :]
    sin_tab = jnp.sin(angles)[:, None, :]
    lower_half = vector[..., :half_dim]
    upper_half = vector[..., half_dim:]
    return jnp.concatenate([lower_half * cos_tab - upper_half * sin_tab, upper_half * cos_tab + lower_half * sin_tab], axis=-1)


def solution(mesh):
    cache_spec = P('dp', 'sp', 'tp', None)
    col_spec = P(None, 'tp')
    row_spec = P('tp', None)
    in_specs = (P(None, 'dp', None), P('dp'), cache_spec, cache_spec, col_spec, col_spec, col_spec, row_spec,
                col_spec, col_spec, row_spec, P(), P(), P(), P())
    out_specs = (P(None, 'dp', None), cache_spec, cache_spec)

    def shard_body(hidden, start_pos, k_cache, v_cache, w_q, w_k, w_v, w_o, w_gate, w_up, w_down, attn_norm, mlp_norm, q_gain, k_gain):
        n_steps, n_batch = hidden.shape[0], hidden.shape[1]
        seq_blk, kv_loc, head_dim = k_cache.shape[1], k_cache.shape[2], k_cache.shape[3]
        heads_loc = w_q.shape[1] // head_dim
        groups = heads_loc // kv_loc
        score_scale = head_dim ** -0.5
        blk_start = lax.axis_index('sp') * seq_blk
        blk_pos = blk_start + jnp.arange(seq_blk)
        old_mask = (blk_pos[None, :] < start_pos[:, None])[:, None, None, :]
        new_keys = []
        new_vals = []
        owned = []
        outputs = []
        for step_idx in range(n_steps):
            tok_pos = start_pos + step_idx
            x_tok = hidden[step_idx]
            normed = rms_scale(x_tok, attn_norm).astype(jnp.bfloat16)
            q_raw = jnp.dot(normed, w_q, preferred_element_type=jnp.float32).reshape(n_batch, heads_loc, head_dim)
            k_raw = jnp.dot(normed, w_k, preferred_element_type=jnp.float32).reshape(n_batch, kv_loc, head_dim)
            v_new = jnp.dot(normed, w_v, preferred_element_type=jnp.float32).astype(jnp.bfloat16).reshape(n_batch, kv_loc, head_dim)
            q_rot = apply_rope(rms_scale(q_raw, q_gain), tok_pos).astype(jnp.bfloat16).reshape(n_batch, kv_loc, groups, head_dim)
            k_new = apply_rope(rms_scale(k_raw, k_gain), tok_pos).astype(jnp.bfloat16)
            new_keys.append(k_new)
            new_vals.append(v_new)
            owned.append((tok_pos >= blk_start) & (tok_pos < blk_start + seq_blk))
            key_stack = jnp.stack(new_keys, axis=1)
            val_stack = jnp.stack(new_vals, axis=1)
            new_mask = jnp.stack(owned, axis=1)[:, None, None, :]
            old_scores = jnp.einsum('bkgh,bskh->bkgs', q_rot, k_cache, preferred_element_type=jnp.float32) * score_scale
            old_scores = jnp.where(old_mask, old_scores, NEG_BIG)
            new_scores = jnp.einsum('bkgh,bjkh->bkgj', q_rot, key_stack, preferred_element_type=jnp.float32) * score_scale
            new_scores = jnp.where(new_mask, new_scores, NEG_BIG)
            blk_max = jnp.maximum(old_scores.max(axis=-1), new_scores.max(axis=-1))
            old_probs = jnp.where(old_mask, jnp.exp(old_scores - blk_max[..., None]), 0.0)
            new_probs = jnp.where(new_mask, jnp.exp(new_scores - blk_max[..., None]), 0.0)
            blk_sum = old_probs.sum(axis=-1) + new_probs.sum(axis=-1)
            blk_out = (jnp.einsum('bkgs,bskh->bkgh', old_probs.astype(jnp.bfloat16), v_cache, preferred_element_type=jnp.float32)
                       + jnp.einsum('bkgj,bjkh->bkgh', new_probs.astype(jnp.bfloat16), val_stack, preferred_element_type=jnp.float32))
            packed = jnp.concatenate([blk_out, blk_max[..., None], blk_sum[..., None]], axis=-1)
            gathered = lax.all_gather(packed, 'sp')
            shard_max = gathered[..., head_dim]
            top_max = shard_max.max(axis=0)
            weights = jnp.exp(shard_max - top_max)
            total = (weights * gathered[..., head_dim + 1]).sum(axis=0)
            attn_vals = (weights[..., None] * gathered[..., :head_dim]).sum(axis=0) / total[..., None]
            attn_in = attn_vals.reshape(n_batch, heads_loc * head_dim).astype(jnp.bfloat16)
            attn_out = lax.psum(jnp.dot(attn_in, w_o, preferred_element_type=jnp.float32), 'tp')
            residual = (x_tok.astype(jnp.float32) + attn_out).astype(jnp.bfloat16)
            mlp_in = rms_scale(residual, mlp_norm).astype(jnp.bfloat16)
            gate_act = jnp.dot(mlp_in, w_gate, preferred_element_type=jnp.float32)
            up_proj = jnp.dot(mlp_in, w_up, preferred_element_type=jnp.float32)
            mlp_act = (jax.nn.silu(gate_act) * up_proj).astype(jnp.bfloat16)
            down_sum = lax.psum(jnp.dot(mlp_act, w_down, preferred_element_type=jnp.float32), 'tp')
            outputs.append((residual.astype(jnp.float32) + down_sum).astype(jnp.bfloat16))
        offsets = blk_pos[None, :] - start_pos[:, None]
        k_out = k_cache
        v_out = v_cache
        for step_idx in range(n_steps):
            hit = (offsets == step_idx)[:, :, None, None]
            k_out = jnp.where(hit, new_keys[step_idx][:, None], k_out)
            v_out = jnp.where(hit, new_vals[step_idx][:, None], v_out)
        return jnp.stack(outputs), k_out, v_out

    return jax.shard_map(shard_body, mesh=mesh, in_specs=in_specs, out_specs=out_specs, check_vma=False)
```

profile of v0, /device:TPU:1, one launch (start us, length us, event | category | flops | bytes accessed | tf_op | source)
XLA Modules:
  0.0 551.1 jit_solution(16883708973383006896)
XLA Ops:
  15.9 3.2 multiply_reduce_fusion.8
  22.5 3.1 multiply_reduce_fusion.10
  26.6 8.1 %copy.544 = bf16[1024,2560]{1,0:T(8,128)(2,1)} copy(bf16[1024,2560]{0,1:T(8,128)(2,1)} %bitcast.261) | data formatting | bytes 10485760 | tf_op jit(solution)/shard_map/dot_general | solution.py:54
  34.8 4.4 multiply_reduce_fusion.4
  58.0 6.5 %fusion.262 = (f32[64,2,4]{2,1,0:T(2,128)S(1)}, f32[64,2,4,256]{3,2,1,0:T(4,128)}) fusion(bf16[64,256,2,128]{3,2,1,0:T(2,128)(2,1)} %param.17, bf16[64,2,4,64]{3,2,1,0:T(4,128)(2,1)S(1)} %copy.492, bf16[64,2,4,64]{3,2,1,0:T(4,128)(2,1)S(1)} %copy.491, pred[64,256]{1,0:T(8,128)(4,1)S(1)} %copy-done.34), kind=kOutput, calls=%fused_computation.381 | convolution fusion | flops 34209280 | bytes 9062400 | tf_op jit(solution)/shard_map/bkgh,bskh->bkgs/dot_general | solution.py:65
  64.6 6.5 %fusion.261 = (f32[64,2,4]{2,1,0:T(2,128)S(1)}, f32[64,2,4,256]{3,2,1,0:T(4,128)}) fusion(bf16[64,256,2,128]{3,2,1,0:T(2,128)(2,1)} %param.17, bf16[64,2,4,64]{3,2,1,0:T(4,128)(2,1)S(1)} %copy.469, bf16[64,2,4,64]{3,2,1,0:T(4,128)(2,1)S(1)} %copy.468, pred[64,256]{1,0:T(8,128)(4,1)S(1)} %copy-done.34), kind=kOutput, calls=%fused_computation.380 | convolution fusion | flops 34209280 | bytes 9062400 | tf_op jit(solution)/shard_map/bkgh,bskh->bkgs/dot_general | solution.py:65
  72.2 6.1 %fusion.258 = (f32[64,2,4]{2,1,0:T(2,128)S(1)}, f32[64,2,4,256]{3,2,1,0:T(4,128)S(1)}) fusion(bf16[64,256,2,128]{3,2,1,0:T(2,128)(2,1)} %param.17, bf16[64,2,4,64]{3,2,1,0:T(4,128)(2,1)S(1)} %copy.437, bf16[64,2,4,64]{3,2,1,0:T(4,128)(2,1)S(1)} %copy.436, pred[64,256]{1,0:T(8,128)(4,1)S(1)} %copy-done.34), kind=kOutput, calls=%fused_computation.377 | convolution fusion | flops 34209280 | bytes 9062400 | tf_op jit(solution)/shard_map/bkgh,bskh->bkgs/dot_general | solution.py:65
  80.4 5.9 %fusion.259 = (f32[64,2,4]{2,1,0:T(2,128)S(1)}, f32[64,2,4,256]{3,2,1,0:T(4,128)S(1)}) fusion(bf16[64,256,2,128]{3,2,1,0:T(2,128)(2,1)} %param.17, bf16[64,2,4,64]{3,2,1,0:T(4,128)(2,1)S(1)} %copy.451, bf16[64,2,4,64]{3,2,1,0:T(4,128)(2,1)S(1)} %copy.450, pred[64,256]{1,0:T(8,128)(4,1)S(1)} %copy-done.35), kind=kOutput, calls=%fused_computation.378 | convolution fusion | flops 34209280 | bytes 9062400 | tf_op jit(solution)/shard_map/bkgh,bskh->bkgs/dot_general | solution.py:65
  88.3 5.4 fusion
  102.8 4.9 fusion.2
  111.6 4.8 fusion.32
  119.7 4.7 fusion.4
  128.5 20.8 %all-gather.13.cloned.1.call-done = f32[256,2,4,130]{3,2,1,0:T(4,128)} async-done(((f32[64,2,4,130]{3,2,1,0:T(4,128)}), f32[256,2,4,130]{3,2,1,0:T(4,128)}) %all-gather.13.cloned.1.call-update) | async-done | bytes 1064976 | tf_op jit(solution)/shard_map/all_gather | solution.py:76
  151.8 21.4 %all-gather.9.cloned.1.call-done = f32[256,2,4,130]{3,2,1,0:T(4,128)} async-done(((f32[64,2,4,130]{3,2,1,0:T(4,128)}), f32[256,2,4,130]{3,2,1,0:T(4,128)}) %all-gather.9.cloned.1.call-update) | async-done | bytes 1064976 | tf_op jit(solution)/shard_map/all_gather | solution.py:76
  175.6 5.9 %fusion.256 = (f32[4,64,2,4,1]{4,3,2,1,0:T(4,128)}, f32[64,2,4]{2,1,0:T(2,128)S(1)}, f32[4,64,2,4,1]{4,3,2,1,0:T(4,128)}, f32[4,64,2,4,1]{4,3,2,1,0:T(4,128)}, f...) fusion(f32[4,64,2,4,130]{4,3,2,1,0:T(4,128)} %bitcast.265, f32[4,64,2,4,130]{4,3,2,1,0:T(4,128)} %bitcast.263), kind=kLoop, calls=%fused_computation.375 | loop fusion | flops 3072 | bytes 69632 | tf_op jit(solution)/shard_map/slice | solution.py:80
  181.5 15.5 %all-gather.11.cloned.1.call-done = f32[256,2,4,130]{3,2,1,0:T(4,128)} async-done(((f32[64,2,4,130]{3,2,1,0:T(4,128)}), f32[256,2,4,130]{3,2,1,0:T(4,128)}) %all-gather.11.cloned.1.call-update) | async-done | bytes 1064976 | tf_op jit(solution)/shard_map/all_gather | solution.py:76
  198.4 6.0 %fusion.254 = (f32[4,64,2,4,1]{4,3,2,1,0:T(4,128)}, f32[64,2,4]{2,1,0:T(2,128)S(1)}, f32[4,64,2,4,1]{4,3,2,1,0:T(4,128)}, f32[4,64,2,4,1]{4,3,2,1,0:T(4,128)}, f...) fusion(f32[4,64,2,4,130]{4,3,2,1,0:T(4,128)} %bitcast.267, f32[4,64,2,4,130]{4,3,2,1,0:T(4,128)} %bitcast.269), kind=kLoop, calls=%fused_computation.373 | loop fusion | flops 3072 | bytes 69632 | tf_op jit(solution)/shard_map/slice | solution.py:80
  216.7 3.2 multiply_reduce_fusion
  220.0 4.5 fusion.266
  237.4 3.1 multiply_reduce_fusion.3
  240.5 4.4 fusion.263
  249.9 4.4 fusion.264
  255.2 101.0 %all-reduce.7.cloned.1.call-done = (f32[64,2560]{1,0:T(8,128)}, f32[64,2560]{1,0:T(8,128)}, f32[64,2560]{1,0:T(8,128)}, f32[64,2560]{1,0:T(8,128)}) async-done(((f32[64,2560]{1,0:T(8,128)}, f32[64,2560]{1,0:T(8,128)}, f32[64,2560]{1,0:T(8,128)}, f32[64,2560]{1,0:T(8,128)}), (f32[64,2560]{1,0:T(8,128)}, f32[64,2560]{1,0:T(8,128)}, f32[64,2560]{1,0:T(8,128)}, ...) | async-done | bytes 2621456 | tf_op jit(solution)/shard_map/psum | solution.py:83
  358.6 7.1 %fusion.186 = f32[64,2432]{1,0:T(8,128)S(1)} fusion(bf16[2560,2432]{1,0:T(8,128)(2,1)} %param.23, bf16[64,2560]{1,0:T(8,128)(2,1)S(1)} %get-tuple-element.47, f32[64]{0:T(128)S(1)} %add_rsqrt_fusion.8, f32[2560]{0:T(1024)S(1)} %convert_element_type.307), kind=kOutput, calls=%fused_computation.242 | convolution fusion | flops 797573120 | bytes 13412608 | tf_op jit(solution)/shard_map/dot_general | solution.py:86
  368.2 13.4 %fusion.100 = f32[64,2560]{1,0:T(8,128)} fusion(bf16[2432,2560]{1,0:T(8,128)(2,1)} %param.25, bf16[2560,2432]{1,0:T(8,128)(2,1)} %param.24, f32[64,2432]{1,0:T(8,128)S(1)} %fusion.186, bf16[64,2560]{1,0:T(8,128)(2,1)S(1)} %get-tuple-element.47, f32[64]{0:T(128)S(1)} %add_rsqrt_fusion.8, f32[2560]{0:T(1024)S(1)} %convert_element_type.307), kind=kOutput, calls=%fused_computation.127 | convolution fusion | flops 1595424768 | bytes 26519808 | tf_op jit(solution)/shard_map/dot_general | solution.py:89
  381.5 13.4 %fusion.104 = f32[64,2560]{1,0:T(8,128)} fusion(bf16[2432,2560]{1,0:T(8,128)(2,1)} %param.25, bf16[2560,2432]{1,0:T(8,128)(2,1)} %param.24, f32[64,2432]{1,0:T(8,128)S(1)} %fusion.190, bf16[64,2560]{1,0:T(8,128)(2,1)S(1)} %get-tuple-element.45, f32[64]{0:T(128)S(1)} %add_rsqrt_fusion.10, f32[2560]{0:T(1024)S(1)} %convert_element_type.307), kind=kOutput, calls=%fused_computation.131 | convolution fusion | flops 1595424768 | bytes 26519808 | tf_op jit(solution)/shard_map/dot_general | solution.py:89
  394.9 7.1 %fusion.194 = f32[64,2432]{1,0:T(8,128)S(1)} fusion(bf16[2560,2432]{1,0:T(8,128)(2,1)} %param.23, bf16[64,2560]{1,0:T(8,128)(2,1)S(1)} %get-tuple-element.43, f32[64]{0:T(128)S(1)} %add_rsqrt_fusion.12, f32[2560]{0:T(1024)S(1)} %convert_element_type.307), kind=kOutput, calls=%fused_computation.244 | convolution fusion | flops 797573120 | bytes 13412608 | tf_op jit(solution)/shard_map/dot_general | solution.py:86
  402.0 13.4 %fusion.108 = f32[64,2560]{1,0:T(8,128)} fusion(bf16[2432,2560]{1,0:T(8,128)(2,1)} %param.25, bf16[2560,2432]{1,0:T(8,128)(2,1)} %param.24, f32[64,2432]{1,0:T(8,128)S(1)} %fusion.194, bf16[64,2560]{1,0:T(8,128)(2,1)S(1)} %get-tuple-element.43, f32[64]{0:T(128)S(1)} %add_rsqrt_fusion.12, f32[2560]{0:T(1024)S(1)} %convert_element_type.307), kind=kOutput, calls=%fused_computation.135 | convolution fusion | flops 1595424768 | bytes 26519808 | tf_op jit(solution)/shard_map/dot_general | solution.py:89
  415.4 6.9 %fusion.198 = f32[64,2432]{1,0:T(8,128)S(1)} fusion(bf16[2560,2432]{1,0:T(8,128)(2,1)} %param.23, bf16[64,2560]{1,0:T(8,128)(2,1)S(1)} %get-tuple-element.20, f32[2560]{0:T(1024)S(1)} %convert_element_type.307, f32[64]{0:T(128)S(1)} %add_rsqrt_fusion.14), kind=kOutput, calls=%fused_computation.245 | convolution fusion | flops 797573120 | bytes 13412608 | tf_op jit(solution)/shard_map/dot_general | solution.py:86
  422.3 13.4 %fusion.112 = f32[64,2560]{1,0:T(8,128)} fusion(bf16[2432,2560]{1,0:T(8,128)(2,1)} %param.25, bf16[2560,2432]{1,0:T(8,128)(2,1)} %param.24, f32[64,2432]{1,0:T(8,128)S(1)} %fusion.198, bf16[64,2560]{1,0:T(8,128)(2,1)S(1)} %get-tuple-element.20, f32[2560]{0:T(1024)S(1)} %convert_element_type.307, f32[64]{0:T(128)S(1)} %add_rsqrt_fusion.14), kind=kOutput, calls=%fused_computation.139 | convolution fusion | flops 1595424768 | bytes 26519808 | tf_op jit(solution)/shard_map/dot_general | solution.py:89
  435.8 77.7 %broadcast_select_fusion.6 = (bf16[64,256,2,128]{3,2,1,0:T(2,128)(2,1)}, bf16[64,256,2,128]{3,2,1,0:T(2,128)(2,1)}) fusion(pred[64,256]{1,0:T(8,128)(4,1)S(1)} %copy-done.31, pred[64,256]{1,0:T(8,128)(4,1)S(1)} %copy-done.33, pred[64,256]{1,0:T(8,128)(4,1)S(1)} %copy-done.32, bf16[64,256,2,128]{3,2,1,0:T(2,128)(2,1)} %param.18, ...), kind=kLoop, calls=%fused_computation.6 | loop fusion | flops 33554432 | bytes 33882112 | tf_op jit(solution)/shard_map/jit(_where)/select_n | solution.py:97
  513.6 24.4 %all-reduce.5.cloned.1.call-done = (f32[64,2560]{1,0:T(8,128)}, f32[64,2560]{1,0:T(8,128)}, f32[64,2560]{1,0:T(8,128)}, f32[64,2560]{1,0:T(8,128)}) async-done(((f32[64,2560]{1,0:T(8,128)}, f32[64,2560]{1,0:T(8,128)}, f32[64,2560]{1,0:T(8,128)}, f32[64,2560]{1,0:T(8,128)}), (f32[64,2560]{1,0:T(8,128)}, f32[64,2560]{1,0:T(8,128)}, f32[64,2560]{1,0:T(8,128)}, ...) | async-done | bytes 2621456 | tf_op jit(solution)/shard_map/psum | solution.py:89
  (310 shorter events, 104.6 us)
Async XLA Ops:
  7.2 8.7 %copy-start.3 = (bf16[4,64,2560]{2,1,0:T(8,128)(2,1)S(1)}, bf16[4,64,2560]{2,1,0:T(8,128)(2,1)}, u32[]{:S(2)}) copy-start(bf16[4,64,2560]{2,1,0:T(8,128)(2,1)} %param.15) | copy-start | bytes 3932164
  7.2 118.9 %all-gather.15.cloned.1.call-start = ((), (), s32[]{:S(2)}) async-start(), calls=%async_computation.3 | async-start | bytes 2621440 | tf_op jit(solution)/shard_map/all_gather | solution.py:76
  15.9 10.1 %copy-start.4 = (bf16[256,2560]{1,0:T(8,128)(2,1)S(1)}, bf16[256,2560]{1,0:T(8,128)(2,1)}, u32[]{:S(2)}) copy-start(bf16[256,2560]{1,0:T(8,128)(2,1)} %copy.545) | copy-start | bytes 3932164
  41.1 8.7 %copy-start.56 = (s32[256]{0:T(256)S(1)}, s32[256]{0:T(256)}, u32[]{:S(2)}) copy-start(s32[256]{0:T(256)} %iota_add_fusion) | copy-start | bytes 3076
  41.1 9.4 %copy-start.53 = (f32[64,2]{0,1:T(2,128)S(1)}, f32[64,2]{0,1:T(2,128)}, u32[]{:S(2)}) copy-start(f32[64,2]{0,1:T(2,128)} %get-tuple-element.113) | copy-start | bytes 1540
  41.1 9.4 %copy-start.54 = (f32[64,2]{0,1:T(2,128)S(1)}, f32[64,2]{0,1:T(2,128)}, u32[]{:S(2)}) copy-start(f32[64,2]{0,1:T(2,128)} %get-tuple-element.117) | copy-start | bytes 1540
  41.1 9.5 %copy-start.55 = (f32[64,2]{0,1:T(2,128)S(1)}, f32[64,2]{0,1:T(2,128)}, u32[]{:S(2)}) copy-start(f32[64,2]{0,1:T(2,128)} %get-tuple-element.115) | copy-start | bytes 1540
  41.1 9.5 %copy-start.57 = (f32[64]{0:T(128)S(1)}, f32[64]{0:T(128)}, u32[]{:S(2)}) copy-start(f32[64]{0:T(128)} %negate_power_fusion) | copy-start | bytes 772
  41.1 10.1 %copy-start.25 = (f32[64,2,128]{2,0,1:T(8,128)S(1)}, f32[64,2,128]{2,0,1:T(8,128)}, u32[]{:S(2)}) copy-start(f32[64,2,128]{2,0,1:T(8,128)} %get-tuple-element.114) | copy-start | bytes 196612
  41.1 10.1 %copy-start.26 = (f32[64,2,128]{2,0,1:T(8,128)S(1)}, f32[64,2,128]{2,0,1:T(8,128)}, u32[]{:S(2)}) copy-start(f32[64,2,128]{2,0,1:T(8,128)} %get-tuple-element.118) | copy-start | bytes 196612
  41.1 10.1 %copy-start.27 = (f32[64,2,128]{2,0,1:T(8,128)S(1)}, f32[64,2,128]{2,0,1:T(8,128)}, u32[]{:S(2)}) copy-start(f32[64,2,128]{2,0,1:T(8,128)} %get-tuple-element.116) | copy-start | bytes 196612
  72.2 8.2 %copy-start.35 = (pred[64,256]{1,0:T(8,128)(4,1)S(1)}, pred[64,256]{1,0:T(8,128)(4,1)}, u32[]{:S(2)}) copy-start(pred[64,256]{1,0:T(8,128)(4,1)} %get-tuple-element.74) | copy-start | bytes 49156
  78.2 15.5 %copy-start.10 = (f32[64,2,4,256]{3,2,1,0:T(4,128)}, f32[64,2,4,256]{3,2,1,0:T(4,128)S(1)}, u32[]{:S(2)}) copy-start(f32[64,2,4,256]{3,2,1,0:T(4,128)S(1)} %get-tuple-element.122) | copy-start | bytes 1572868
  78.3 8.0 %copy-start.39 = (bf16[64,2,2,128]{3,0,2,1:T(8,128)(2,1)S(1)}, bf16[64,2,2,128]{3,0,2,1:T(8,128)(2,1)}, u32[]{:S(2)}) copy-start(bf16[64,2,2,128]{3,0,2,1:T(8,128)(2,1)} %maximum_maximum_fusion.2) | copy-start | bytes 196612
  78.3 8.0 %copy-start.46 = (pred[64,2]{1,0:T(8,128)(4,1)S(1)}, pred[64,2]{1,0:T(8,128)(4,1)}, u32[]{:S(2)}) copy-start(pred[64,2]{1,0:T(8,128)(4,1)} %copy.453) | copy-start | bytes 388
  99.8 49.5 %all-gather.13.cloned.1.call-start = ((), (), s32[]{:S(2)}) async-start(), calls=%async_computation.2 | async-start | bytes 2621440 | tf_op jit(solution)/shard_map/all_gather | solution.py:76
  102.8 8.7 %copy-start.37 = (pred[64,256]{1,0:T(8,128)(4,1)S(1)}, pred[64,256]{1,0:T(8,128)(4,1)}, u32[]{:S(2)}) copy-start(pred[64,256]{1,0:T(8,128)(4,1)} %get-tuple-element.74) | copy-start | bytes 49156
  102.8 8.7 %copy-start.38 = (f32[64,2,4]{2,1,0:T(2,128)S(1)}, f32[64,2,4]{2,1,0:T(2,128)}, u32[]{:S(2)}) copy-start(f32[64,2,4]{2,1,0:T(2,128)} %get-tuple-element.27) | copy-start | bytes 6148
  109.1 64.1 %all-gather.9.cloned.1.call-start = ((), (), s32[]{:S(2)}) async-start(), calls=%async_computation | async-start | bytes 2621440 | tf_op jit(solution)/shard_map/all_gather | solution.py:76
  117.5 79.5 %all-gather.11.cloned.1.call-start = ((), (), s32[]{:S(2)}) async-start(), calls=%async_computation.1 | async-start | bytes 2621440 | tf_op jit(solution)/shard_map/all_gather | solution.py:76
  126.0 230.1 %all-reduce.7.cloned.1.call-start = ((), (), s32[]{:S(2)}) async-start(), calls=%async_computation.5 | async-start | bytes 5242880 | tf_op jit(solution)/shard_map/psum | solution.py:83
  254.3 283.7 %all-reduce.5.cloned.1.call-start = ((), (), s32[]{:S(2)}) async-start(), calls=%async_computation.4 | async-start | bytes 5242880 | tf_op jit(solution)/shard_map/psum | solution.py:89
  356.2 9.6 %slice-start = ((s8[12451840]{0:T(1024)(128)(4,1)}), s8[4194304]{0:T(1024)(128)(4,1)S(1)}, s32[]{:S(2)}) async-start(s8[12451840]{0:T(1024)(128)(4,1)} %bitcast.249), calls=%async_computation.6 | async-start | bytes 8388608
  358.5 43.5 %copy-start.6 = (bf16[64,2560]{1,0:T(8,128)(2,1)}, bf16[64,2560]{1,0:T(8,128)(2,1)S(1)}, u32[]{:S(2)}) copy-start(bf16[64,2560]{1,0:T(8,128)(2,1)S(1)} %get-tuple-element.43) | copy-start | bytes 983044
  358.6 63.7 %copy-start.8 = (bf16[64,2560]{1,0:T(8,128)(2,1)}, bf16[64,2560]{1,0:T(8,128)(2,1)S(1)}, u32[]{:S(2)}) copy-start(bf16[64,2560]{1,0:T(8,128)(2,1)S(1)} %get-tuple-element.20) | copy-start | bytes 983044
  422.3 13.5 %copy-start.30 = (pred[64,256]{1,0:T(8,128)(4,1)S(1)}, pred[64,256]{1,0:T(8,128)(4,1)}, u32[]{:S(2)}) copy-start(pred[64,256]{1,0:T(8,128)(4,1)} %get-tuple-element.70) | copy-start | bytes 49156
  422.3 13.5 %copy-start.31 = (pred[64,256]{1,0:T(8,128)(4,1)S(1)}, pred[64,256]{1,0:T(8,128)(4,1)}, u32[]{:S(2)}) copy-start(pred[64,256]{1,0:T(8,128)(4,1)} %get-tuple-element.71) | copy-start | bytes 49156
  422.3 13.5 %copy-start.32 = (pred[64,256]{1,0:T(8,128)(4,1)S(1)}, pred[64,256]{1,0:T(8,128)(4,1)}, u32[]{:S(2)}) copy-start(pred[64,256]{1,0:T(8,128)(4,1)} %get-tuple-element.72) | copy-start | bytes 49156
  422.3 13.5 %copy-start.33 = (pred[64,256]{1,0:T(8,128)(4,1)S(1)}, pred[64,256]{1,0:T(8,128)(4,1)}, u32[]{:S(2)}) copy-start(pred[64,256]{1,0:T(8,128)(4,1)} %get-tuple-element.73) | copy-start | bytes 49156
  435.8 102.2 %copy-start.9 = (bf16[64,2560]{1,0:T(8,128)(2,1)S(1)}, bf16[64,2560]{1,0:T(8,128)(2,1)}, u32[]{:S(2)}) copy-start(bf16[64,2560]{1,0:T(8,128)(2,1)} %copy-done.8) | copy-start | bytes 983044
  435.8 103.3 %copy-start.7 = (bf16[64,2560]{1,0:T(8,128)(2,1)S(1)}, bf16[64,2560]{1,0:T(8,128)(2,1)}, u32[]{:S(2)}) copy-start(bf16[64,2560]{1,0:T(8,128)(2,1)} %copy-done.6) | copy-start | bytes 983044
  435.8 108.0 %copy-start.1 = (bf16[2560,256]{1,0:T(8,128)(2,1)S(1)}, bf16[2560,256]{1,0:T(8,128)(2,1)}, u32[]{:S(2)}) copy-start(bf16[2560,256]{1,0:T(8,128)(2,1)} %param.21) | copy-start | bytes 3932164
  (39 other events, 202.4 us)
Sparse Core Ops, SparseCore 0:
  100.0 24.7 all-gather.14
  126.9 22.3 all-gather.12
  150.9 22.3 all-gather.8
  174.6 22.3 all-gather.10
  254.4 101.7 all-reduce.6
  435.9 102.0 all-reduce.4
where the time goes:
time: 557 us; the launch traced here: 551 us
  waiting for transfers between devices  183 us (33%)
  matrix products  165 us (30%)
  other arithmetic  129 us (23%)
  local copies, waits for them, and re-layouts  56.8 us (10%)
  between operations  16 us (3%)
    psum x1, waiting for transfers between devices, shard_body(): lax.psum(jnp.dot(attn_in, w_o, preferred_element_type=jnp.float32), 'tp')  101 us
    select_n x1, other arithmetic, shard_body(): v_out = jnp.where(hit, new_vals[step_idx][:, None], v_out)  77.7 us
    all_gather x4, waiting for transfers between devices, shard_body(): gathered = lax.all_gather(packed, 'sp')  57.8 us
    dot_general x4, matrix products, shard_body(): jnp.dot(mlp_act, w_down, preferred_element_type=jnp.float32)  53.5 us
    dot_general x4, matrix products, shard_body(): jnp.einsum('bkgh,bskh->bkgs', q_rot, k_cache, preferred_element_type=jnp....  25 us
    psum x1, waiting for transfers between devices, shard_body(): lax.psum(jnp.dot(mlp_act, w_down, preferred_element_type=jnp.float32), 'tp')  24.4 us
    unnamed x150, local copies, waits for them, and re-layouts  24.2 us
    dot_general x4, matrix products, shard_body(): gate_act = jnp.dot(mlp_in, w_gate, preferred_element_type=jnp.float32)  23.4 us
  transfers between devices with their start and end apart: 6, of which 5 were waited for; matrix products, arithmetic and copies ran while one was open for 21% of the time, Pallas kernels for 0%

commit v1 on v0

v1 whole, which is shorter than its diff:
```python
import functools
import jax
import jax.numpy as jnp
from jax import lax
from jax.experimental import pallas as pl
from jax.experimental.pallas import tpu as pltpu
from jax.sharding import PartitionSpec as P

ROPE_BASE = 1000000.0
NORM_EPS = 1e-06
NEG = -3.0e38
F32 = jnp.float32
BF16 = jnp.bfloat16
MESH = pl.DeviceIdType.MESH
STATS = 128
GROUP = 4
PIECE = 256
LAG = 2
VMEM_LIMIT = 66_900_000


def dot(a, b):
    return jnp.dot(a, b, preferred_element_type=F32)


def attn_kernel(start_ref, hid_ref, cos_ref, sin_ref, norm_ref, qg_ref, kg_ref, wq_ref, wk_ref, wv_ref, kc_ref, vc_ref,
                o_ref, ko_ref, vo_ref,
                hid, normed, wq, wk, wv, kbuf, vbuf, qs, ks, vs, ostage, thr, hid_sem, w_sem, in_sem, out_sem, o_sem):
    n_rows, d_model = hid.shape
    n_batch, rows_kv, hd = kbuf.shape
    n_steps = n_rows // n_batch
    heads = wq.shape[1] // hd
    kv = wk.shape[1] // hd
    seq = rows_kv // kv
    n_groups = n_batch // GROUP
    qrows = heads * n_steps
    blk_start = lax.axis_index('sp') * seq

    hid_cp = pltpu.make_async_copy(hid_ref, hid, hid_sem)
    hid_cp.start()
    n_q = wq.shape[1] // 256
    w_cps = []
    for i in range(n_q):
        w_cps.append(pltpu.make_async_copy(wq_ref.at[:, pl.ds(i * 256, 256)], wq.at[:, pl.ds(i * 256, 256)], w_sem.at[i]))
    w_cps.append(pltpu.make_async_copy(wk_ref, wk, w_sem.at[n_q]))
    w_cps.append(pltpu.make_async_copy(wv_ref, wv, w_sem.at[n_q + 1]))
    for cp in w_cps:
        cp.start()

    def cache_in(g, which):
        src, dst = ((kc_ref, kbuf), (vc_ref, vbuf))[which]
        rows = pl.ds(g * GROUP, GROUP)
        return pltpu.make_async_copy(src.at[rows], dst.at[rows], in_sem.at[which, g])

    def cache_out(g, which):
        src, dst = ((kbuf, ko_ref), (vbuf, vo_ref))[which]
        rows = pl.ds(g * GROUP, GROUP)
        return pltpu.make_async_copy(src.at[rows], dst.at[rows], out_sem.at[which, g])

    def o_out(g):
        rows = pl.ds(pl.multiple_of(g * GROUP * n_steps, GROUP * n_steps), GROUP * n_steps)
        return pltpu.make_async_copy(ostage.at[rows], o_ref.at[rows], o_sem.at[g])

    def start_in(g, c):
        cache_in(g, 0).start()
        cache_in(g, 1).start()
        return c

    lax.fori_loop(0, n_groups, start_in, 0)

    ri = lax.broadcasted_iota(jnp.int32, (qrows, rows_kv), 0)
    ci = lax.broadcasted_iota(jnp.int32, (qrows, rows_kv), 1)
    row_kv = ri // (qrows // kv)
    thr[...] = jnp.where(ci % kv == row_kv, ci - kv * (ri % n_steps), 1 << 24)

    hid_cp.wait()
    gain = norm_ref[...].astype(F32)
    chunk = 32

    def norm_rows(i, c):
        rows = pl.ds(pl.multiple_of(i * chunk, chunk), chunk)
        x = hid[rows, :].astype(F32)
        inv = lax.rsqrt(jnp.mean(x * x, axis=-1, keepdims=True) + NORM_EPS)
        normed[rows, :] = (x * inv * gain).astype(BF16)
        return c

    lax.fori_loop(0, n_rows // chunk, norm_rows, 0)

    pi = lax.broadcasted_iota(jnp.int32, (n_rows, n_rows), 0)
    pj = lax.broadcasted_iota(jnp.int32, (n_rows, n_rows), 1)
    perm = jnp.where(pj == (pi % n_steps) * n_batch + pi // n_steps, 1.0, 0.0).astype(BF16)

    def norm_rope(x, g):
        inv = lax.rsqrt(jnp.mean(x * x, axis=-1, keepdims=True) + NORM_EPS)
        x = x * inv * g
        return x * cos_ref[...] + pltpu.roll(x, hd // 2, 1) * sin_ref[...]

    qg = qg_ref[...].astype(F32)
    kg = kg_ref[...].astype(F32)
    for i in range(n_q + 2):
        w_cps[i].wait()
        if i < n_q:
            raw = dot(normed[...], wq[:, i * 256:(i + 1) * 256])
        elif i == n_q:
            raw = dot(normed[...], wk[...])
        else:
            raw = dot(normed[...], wv[...])
        if i <= n_q:
            g = qg if i < n_q else kg
            raw = jnp.concatenate([norm_rope(raw[:, :hd], g), norm_rope(raw[:, hd:], g)], axis=1)
        done = dot(perm, raw.astype(BF16))
        if i < n_q:
            qs[:, i * 256:(i + 1) * 256] = done
        elif i == n_q:
            ks[...] = done
        else:
            vs[...] = done

    scale = hd ** -0.5
    grows = GROUP * n_steps
    lane = lax.broadcasted_iota(jnp.int32, (grows, STATS), 1)
    win_rows = lax.broadcasted_iota(jnp.int32, (32, hd), 0)

    def group_step(g, c):
        cache_in(g, 0).wait()
        cache_in(g, 1).wait()
        rows = pl.ds(pl.multiple_of(g * grows, grows), grows)
        q_slab = qs[rows, :]
        k_slab = ks[rows, :]
        v_slab = vs[rows, :]
        outs, maxes, sums = [], [], []
        for r in range(GROUP):
            b = g * GROUP + r
            off = kv * (start_ref[b] - blk_start)
            win = pl.multiple_of(jnp.clip((off // 16) * 16, 0, rows_kv - 32), 16)
            for buf, slab in ((kbuf, k_slab), (vbuf, v_slab)):
                cur = buf[b, pl.ds(win, 32), :].astype(F32)
                for j in range(n_steps):
                    for h in range(kv):
                        new = slab[r * n_steps + j:r * n_steps + j + 1, h * hd:(h + 1) * hd]
                        cur = jnp.where(win_rows == off + kv * j + h - win, new, cur)
                buf[b, pl.ds(win, 32), :] = cur.astype(BF16)
            q = jnp.concatenate([q_slab[r * n_steps:(r + 1) * n_steps, h * hd:(h + 1) * hd] for h in range(heads)], axis=0)
            s = lax.dot_general(q.astype(BF16), kbuf[b], (((1,), (1,)), ((), ())), preferred_element_type=F32) * scale
            keep = thr[...] <= off + kv - 1
            s = jnp.where(keep, s, NEG)
            m = jnp.max(s, axis=-1, keepdims=True)
            p = jnp.where(keep, jnp.exp(s - m), 0.0)
            sums.append(jnp.sum(p, axis=-1, keepdims=True))
            maxes.append(m)
            outs.append(dot(p.astype(BF16), vbuf[b]))
        stats = jnp.zeros((grows, STATS), F32)
        for h in range(heads):
            sl = slice(h * n_steps, (h + 1) * n_steps)
            ostage[rows, h * hd:(h + 1) * hd] = jnp.concatenate([o[sl] for o in outs], axis=0)
            stats = jnp.where(lane == h, jnp.concatenate([m[sl] for m in maxes], axis=0), stats)
            stats = jnp.where(lane == heads + h, jnp.concatenate([t[sl] for t in sums], axis=0), stats)
        ostage[rows, heads * hd:] = stats
        cache_out(g, 0).start()
        cache_out(g, 1).start()
        o_out(g).start()
        return c

    lax.fori_loop(0, n_groups, group_step, 0)

    def drain(g, c):
        cache_out(g, 0).wait()
        cache_out(g, 1).wait()
        o_out(g).wait()
        return c

    lax.fori_loop(0, n_groups, drain, 0)


def attention(start_pos, hidden, cos, sin, attn_norm, q_gain, k_gain, w_q, w_k, w_v, k_cache, v_cache):
    n_rows, d_model = hidden.shape
    n_batch, rows_kv, hd = k_cache.shape
    heads = w_q.shape[1] // hd
    n_groups = n_batch // GROUP
    n_steps = n_rows // n_batch
    n_w = w_q.shape[1] // 256 + 2
    width = heads * hd + STATS
    vmem = pl.BlockSpec(memory_space=pltpu.VMEM)
    hbm = pl.BlockSpec(memory_space=pl.ANY)
    return pl.pallas_call(
        attn_kernel,
        out_shape=(jax.ShapeDtypeStruct((n_rows, width), F32),
                   jax.ShapeDtypeStruct(k_cache.shape, BF16), jax.ShapeDtypeStruct(v_cache.shape, BF16)),
        in_specs=[pl.BlockSpec(memory_space=pltpu.SMEM), hbm, vmem, vmem, vmem, vmem, vmem, hbm, hbm, hbm, hbm, hbm],
        out_specs=(hbm, hbm, hbm),
        scratch_shapes=[
            pltpu.VMEM((n_rows, d_model), BF16), pltpu.VMEM((n_rows, d_model), BF16),
            pltpu.VMEM(w_q.shape, BF16), pltpu.VMEM(w_k.shape, BF16), pltpu.VMEM(w_v.shape, BF16),
            pltpu.VMEM(k_cache.shape, BF16), pltpu.VMEM(v_cache.shape, BF16),
            pltpu.VMEM((n_rows, w_q.shape[1]), F32), pltpu.VMEM((n_rows, w_k.shape[1]), F32),
            pltpu.VMEM((n_rows, w_v.shape[1]), F32), pltpu.VMEM((n_rows, width), F32),
            pltpu.VMEM((heads * n_steps, rows_kv), jnp.int32),
            pltpu.SemaphoreType.DMA, pltpu.SemaphoreType.DMA((n_w,)),
            pltpu.SemaphoreType.DMA((2, n_groups)), pltpu.SemaphoreType.DMA((2, n_groups)),
            pltpu.SemaphoreType.DMA((n_groups,)),
        ],
        compiler_params=pltpu.CompilerParams(vmem_limit_bytes=60_000_000),
        name="attn",
    )(start_pos, hidden, cos, sin, attn_norm, q_gain, k_gain, w_q, w_k, w_v, k_cache, v_cache)


def mlp_kernel(o_ref, hid_ref, norm_ref, wo_ref, wg_ref, wu_ref, wd_ref,
               out_ref,
               x, wo, wg, wu, wd, loc, dbuf, ysend, yrecv, attn, pbuf, in_leaf, in_mid, tbuf, rbuf, mlp_in, act, fbuf, fy, fd,
               x_sem, w_sem, l_sem, d_ssem, d_rsem, y_ssem, y_rsem,
               up_s, up_r, mid_s, mid_r, dn_s, dn_r, fy_s, fy_r, fd_s, fd_r):
    me = lax.axis_index('sp')
    tp = lax.axis_index('tp')
    core = me % 2
    mate = me + 1 - 2 * core
    oth = (me + 2) % 4
    mate_oth = (mate + 2) % 4
    side = tp + 1 - 2 * (tp % 2)
    mid = 3 - tp
    inner = jnp.logical_or(tp == 1, tp == 2)
    leaf = jnp.logical_or(tp == 0, tp == 3)

    n_pieces, n_rows, _ = rbuf.shape
    width = loc.shape[2]
    hd = 128
    heads = (width - STATS) // hd
    n_chunks = dbuf.shape[1]
    crows = dbuf.shape[2]
    n_steps = out_ref.shape[0]
    n_req = n_rows // n_steps

    w_cps = [pltpu.make_async_copy(s, d, w_sem.at[i]) for i, (s, d) in
             enumerate(((wo_ref, wo), (wg_ref, wg), (wu_ref, wu), (wd_ref, wd)))]
    l_cps = [pltpu.make_async_copy(o_ref.at[oth], loc.at[0], l_sem.at[0]),
             pltpu.make_async_copy(o_ref.at[me], loc.at[1], l_sem.at[1])]
    x_cps = [pltpu.make_async_copy(hid_ref.at[i, pl.ds(pl.multiple_of(me * n_req, n_req), n_req), :],
                                   x.at[pl.ds(i * n_req, n_req), :], x_sem.at[i]) for i in range(n_steps)]
    for cp in l_cps:
        cp.start()
    w_cps[0].start()
    for cp in x_cps:
        cp.start()
    for cp in w_cps[1:]:
        cp.start()

    barrier = pltpu.get_barrier_semaphore()
    for dev in ({'sp': mate}, {'sp': oth}, {'tp': side}):
        pl.semaphore_signal(barrier, inc=1, device_id=dev, device_id_type=MESH)

    @pl.when(inner)
    def _():
        pl.semaphore_signal(barrier, inc=1, device_id={'tp': mid}, device_id_type=MESH)
        pl.semaphore_wait(barrier, 4)

    @pl.when(leaf)
    def _():
        pl.semaphore_wait(barrier, 3)

    def remote(src, dst, ssem, rsem, dev):
        return pltpu.make_async_remote_copy(src_ref=src, dst_ref=dst, send_sem=ssem, recv_sem=rsem,
                                            device_id=dev, device_id_type=MESH)

    def d_copy(which, i):
        blk = (mate_oth, mate)[which]
        return remote(o_ref.at[blk, pl.ds(i * crows, crows), :], dbuf.at[which, i], d_ssem.at[which, i], d_rsem.at[which, i],
                      {'sp': mate})

    def y_copy(i):
        return remote(ysend.at[i], yrecv.at[i], y_ssem.at[i], y_rsem.at[i], {'sp': oth})

    for which in range(2):
        for i in range(n_chunks):
            d_copy(which, i).start()

    aw = heads * hd

    def weights(sa, sb):
        m = jnp.maximum(sa, sb)
        ea = jnp.exp(sa - m)
        eb = jnp.exp(sb - m)
        tot = ea * pltpu.roll(sa, STATS - heads, 1) + eb * pltpu.roll(sb, STATS - heads, 1)
        return m, ea, eb, tot

    def pack_stats(m, tot):
        lane = lax.broadcasted_iota(jnp.int32, m.shape, 1)
        return jnp.where(lane < heads, m, pltpu.roll(tot, heads, 1))

    def merge(a, ai, b, bi, dst, di):
        m, ea, eb, tot = weights(a[ai + (slice(aw, None),)], b[bi + (slice(aw, None),)])
        for h in range(heads):
            sl = (slice(h * hd, (h + 1) * hd),)
            dst[di + sl] = a[ai + sl] * ea[:, h:h + 1] + b[bi + sl] * eb[:, h:h + 1]
        dst[di + (slice(aw, None),)] = pack_stats(m, tot)

    l_cps[0].wait()
    for i in range(n_chunks):
        d_copy(0, i).wait_recv()
        rs = slice(i * crows, (i + 1) * crows)
        merge(loc, (0, rs), dbuf, (0, i, slice(None)), ysend, (i, slice(None)))
        y_copy(i).start()
    l_cps[1].wait()
    for i in range(n_chunks):
        d_copy(1, i).wait_recv()
        rs = slice(i * crows, (i + 1) * crows)
        merge(loc, (1, rs), dbuf, (1, i, slice(None)), loc, (1, rs))
    for i in range(n_chunks):
        y_copy(i).wait_recv()
        rs = slice(i * crows, (i + 1) * crows)
        m, ea, eb, tot = weights(loc[1, rs, aw:], yrecv[i, :, aw:])
        for h in range(heads):
            sl = slice(h * hd, (h + 1) * hd)
            val = loc[1, rs, sl] * ea[:, h:h + 1] + yrecv[i, :, sl] * eb[:, h:h + 1]
            attn[rs, sl] = (val / tot[:, h:h + 1]).astype(BF16)

    pi = lax.broadcasted_iota(jnp.int32, (n_rows, n_rows), 0)
    pj = lax.broadcasted_iota(jnp.int32, (n_rows, n_rows), 1)
    perm = jnp.where(pj == (pi % n_req) * n_steps + pi // n_req, 1.0, 0.0).astype(BF16)
    attn[...] = dot(perm, attn[...]).astype(BF16)

    def up(a, k):
        return remote(pbuf.at[a, k], in_leaf.at[a, k], up_s.at[a, k], up_r.at[a, k], {'tp': side})

    def across(a, k):
        return remote(pbuf.at[a, k], in_mid.at[a, k], mid_s.at[a, k], mid_r.at[a, k], {'tp': mid})

    def down(a, k):
        return remote(tbuf.at[a, k], tbuf.at[a, k], dn_s.at[a, k], dn_r.at[a, k], {'tp': side})

    def all_reduce(a, part, finish):
        @pl.when(leaf)
        def _():
            def send(k, c):
                pbuf[a, k] = part(k)
                up(a, k).start()
                return c
            lax.fori_loop(0, n_pieces, send, 0)

            def take(k, c):
                down(a, k).wait_recv()
                finish(k)
                return c
            lax.fori_loop(0, n_pieces, take, 0)

        @pl.when(inner)
        def _():
            def stage_a(k):
                mine = part(k)
                up(a, k).wait_recv()
                pbuf[a, k] = mine + in_leaf[a, k]
                across(a, k).start()

            def stage_b(k):
                across(a, k).wait_recv()
                tbuf[a, k] = pbuf[a, k] + in_mid[a, k]
                down(a, k).start()
                finish(k)

            for k in range(LAG):
                stage_a(k)

            def body(k, c):
                stage_a(k)
                stage_b(k - LAG)
                return c
            lax.fori_loop(LAG, n_pieces, body, 0)
            for k in range(n_pieces - LAG, n_pieces):
                stage_b(k)

    def cols(k):
        return pl.ds(pl.multiple_of(k * PIECE, PIECE), PIECE)

    w_cps[0].wait()
    for cp in x_cps:
        cp.wait()

    def take_r(k):
        r = (x[:, cols(k)].astype(F32) + tbuf[0, k]).astype(BF16).astype(F32)
        rbuf[k] = r

    all_reduce(0, lambda k: dot(attn[...], wo[:, cols(k)]), take_r)

    sq = jnp.zeros((n_rows, 128), F32)
    for k in range(n_pieces):
        r = rbuf[k]
        for j in range(PIECE // 128):
            piece = r[:, j * 128:(j + 1) * 128]
            sq = sq + piece * piece
    d_model = n_pieces * PIECE
    inv = lax.rsqrt(jnp.sum(sq, axis=-1, keepdims=True) * (1.0 / d_model) + NORM_EPS)
    for k in range(n_pieces):
        g = norm_ref[:, k * PIECE:(k + 1) * PIECE].astype(F32)
        mlp_in[:, k * PIECE:(k + 1) * PIECE] = (rbuf[k] * inv * g).astype(BF16)

    w_cps[1].wait()
    w_cps[2].wait()
    ffn = wg.shape[1]
    wide = 256

    def gate_up(sl):
        gate = dot(mlp_in[...], wg[:, sl])
        upv = dot(mlp_in[...], wu[:, sl])
        act[:, sl] = (gate * (1.0 / (1.0 + jnp.exp(-gate))) * upv).astype(BF16)

    def gu_body(j, c):
        gate_up(pl.ds(pl.multiple_of(j * wide, wide), wide))
        return c
    lax.fori_loop(0, ffn // wide, gu_body, 0)
    if ffn % wide:
        gate_up(pl.ds(ffn // wide * wide, ffn % wide))

    w_cps[3].wait()

    def put(blk, k, val):
        val = val.astype(BF16)
        for i in range(n_steps):
            out_ref[i, pl.ds(pl.multiple_of(blk * n_req, n_req), n_req), cols(k)] = val[i * n_req:(i + 1) * n_req]

    def f_y(k):
        return remote(fbuf.at[k], fy.at[k], fy_s.at[k], fy_r.at[k], {'sp': oth})

    def f_d(which, k):
        src = (fbuf, fy)[which]
        return remote(src.at[k], fd.at[which, k], fd_s.at[which, k], fd_r.at[which, k], {'sp': mate})

    def forward(k):
        f_y(k).wait_recv()
        f_d(1, k).start()
        put(oth, k, fy[k])

    def finish_out(k):
        val = (rbuf[k] + tbuf[1, k]).astype(BF16)
        fbuf[k] = val.astype(F32)
        f_y(k).start()
        f_d(0, k).start()
        put(me, k, val)

        if isinstance(k, int):
            if k >= LAG:
                forward(k - LAG)
        else:
            @pl.when(k >= LAG)
            def _():
                forward(k - LAG)

    all_reduce(1, lambda k: dot(act[...], wd[:, cols(k)]), finish_out)
    for k in range(n_pieces - LAG, n_pieces):
        forward(k)

    def last(k, c):
        f_d(0, k).wait_recv()
        put(mate, k, fd[0, k])
        f_d(1, k).wait_recv()
        put(mate_oth, k, fd[1, k])
        return c
    lax.fori_loop(0, n_pieces, last, 0)

    for which in range(2):
        for i in range(n_chunks):
            d_copy(which, i).wait_send()
    for i in range(n_chunks):
        y_copy(i).wait_send()

    def sends(k, c):
        f_y(k).wait_send()
        f_d(0, k).wait_send()
        f_d(1, k).wait_send()
        for a in range(2):
            @pl.when(leaf)
            def _():
                up(a, k).wait_send()

            @pl.when(inner)
            def _():
                across(a, k).wait_send()
                down(a, k).wait_send()
        return c
    lax.fori_loop(0, n_pieces, sends, 0)


def mlp(o_part, hidden, mlp_norm, w_o, w_gate, w_up, w_down):
    n_blk, n_rows, width = o_part.shape
    n_steps, n_batch, d_model = hidden.shape
    n_pieces = d_model // PIECE
    n_chunks = 4
    crows = n_rows // n_chunks
    ffn = w_gate.shape[1]
    vmem = pl.BlockSpec(memory_space=pltpu.VMEM)
    hbm = pl.BlockSpec(memory_space=pl.ANY)
    dma = pltpu.SemaphoreType.DMA
    piece = (n_pieces, n_rows, PIECE)
    return pl.pallas_call(
        mlp_kernel,
        out_shape=jax.ShapeDtypeStruct(hidden.shape, BF16),
        in_specs=[hbm, hbm, vmem, hbm, hbm, hbm, hbm],
        out_specs=vmem,
        scratch_shapes=[
            pltpu.VMEM((n_rows, d_model), BF16),
            pltpu.VMEM(w_o.shape, BF16), pltpu.VMEM(w_gate.shape, BF16),
            pltpu.VMEM(w_up.shape, BF16), pltpu.VMEM(w_down.shape, BF16),
            pltpu.VMEM((2, n_rows, width), F32), pltpu.VMEM((2, n_chunks, crows, width), F32),
            pltpu.VMEM((n_chunks, crows, width), F32), pltpu.VMEM((n_chunks, crows, width), F32),
            pltpu.VMEM((n_rows, w_o.shape[0]), BF16),
            pltpu.VMEM((2,) + piece, F32), pltpu.VMEM((2,) + piece, F32),
            pltpu.VMEM((2,) + piece, F32), pltpu.VMEM((2,) + piece, F32),
            pltpu.VMEM(piece, F32), pltpu.VMEM((n_rows, d_model), BF16), pltpu.VMEM((n_rows, ffn), BF16),
            pltpu.VMEM(piece, F32), pltpu.VMEM(piece, F32), pltpu.VMEM((2,) + piece, F32),
            dma((n_steps,)), dma((4,)), dma((2,)),
            dma((2, n_chunks)), dma((2, n_chunks)), dma((n_chunks,)), dma((n_chunks,)),
            dma((2, n_pieces)), dma((2, n_pieces)), dma((2, n_pieces)), dma((2, n_pieces)),
            dma((2, n_pieces)), dma((2, n_pieces)),
            dma((n_pieces,)), dma((n_pieces,)), dma((2, n_pieces)), dma((2, n_pieces)),
        ],
        compiler_params=pltpu.CompilerParams(vmem_limit_bytes=VMEM_LIMIT, collective_id=0, has_side_effects=True),
        name="combine_mlp",
    )(o_part, hidden, mlp_norm, w_o, w_gate, w_up, w_down)


def solution(mesh):
    cache_spec = P('dp', 'sp', 'tp', None)
    col_spec = P(None, 'tp')
    row_spec = P('tp', None)
    in_specs = (P(None, 'dp', None), P('dp'), cache_spec, cache_spec, col_spec, col_spec, col_spec, row_spec,
                col_spec, col_spec, row_spec, P(), P(), P(), P())
    out_specs = (P(None, 'dp', None), cache_spec, cache_spec)

    def shard_body(hidden, start_pos, k_cache, v_cache, w_q, w_k, w_v, w_o, w_gate, w_up, w_down, attn_norm, mlp_norm, q_gain, k_gain):
        n_steps, n_batch, d_model = hidden.shape
        _, seq, kv, hd = k_cache.shape
        half = hd // 2
        freqs = ROPE_BASE ** (-(jnp.arange(half, dtype=F32) * (2.0 / hd)))
        tok_pos = (start_pos[None, :] + jnp.arange(n_steps)[:, None]).reshape(-1)
        angles = tok_pos.astype(F32)[:, None] * freqs[None, :]
        cos, sin = jnp.cos(angles), jnp.sin(angles)
        cos = jnp.concatenate([cos, cos], axis=1)
        sin = jnp.concatenate([-sin, sin], axis=1)
        o_part, k_out, v_out = attention(
            start_pos, hidden.reshape(-1, d_model), cos, sin, attn_norm[None], q_gain[None], k_gain[None],
            w_q, w_k, w_v, k_cache.reshape(n_batch, seq * kv, hd), v_cache.reshape(n_batch, seq * kv, hd))
        n_sp = 4
        out = mlp(o_part.reshape(n_sp, -1, o_part.shape[1]), hidden, mlp_norm[None], w_o, w_gate, w_up, w_down)
        return out, k_out.reshape(k_cache.shape), v_out.reshape(v_cache.shape)

    return jax.shard_map(shard_body, mesh=mesh, in_specs=in_specs, out_specs=out_specs, check_vma=False)
```

time: 557 us -> 125 us (0.22)
  waiting for transfers between devices: 183 us -> 0 us
  matrix products: 165 us -> 0 us
  other arithmetic: 129 us -> 2.03 us
  Pallas kernels: 0 us -> 117 us
  local copies, waits for them, and re-layouts: 56.8 us -> 5.12 us
  between operations: 16 us -> 0.66 us
    dot_general x39 -> x0, matrix products: 165 us -> none  [the longest x4 53.5 us: shard_body(): jnp.dot(mlp_act, w_down, preferred_element_type=jnp.float32)]
    psum x2 -> x0, waiting for transfers between devices: 125 us -> none  [the longest x1 101 us: shard_body(): lax.psum(jnp.dot(attn_in, w_o, preferred_element_type=jnp.float32), 'tp')]
    pallas_call x0 -> x2, Pallas kernels: none -> 117 us  [the longest x1 83.2 us: mlp(): pl.pallas_call(mlp_kernel, out_shape=jax.ShapeDtypeStruct(hidden.shape, B...]
    select_n x1 -> x0, other arithmetic: 77.7 us -> none  [shard_body(): v_out = jnp.where(hit, new_vals[step_idx][:, None], v_out)]
    all_gather x4 -> x0, waiting for transfers between devices: 57.8 us -> none  [shard_body(): gathered = lax.all_gather(packed, 'sp')]
    unnamed x150 -> x1, local copies, waits for them, and re-layouts: 24.2 us -> 2.46 us
    reduce_sum x12 -> x0, other arithmetic: 17 us -> none  [the longest x4 10.8 us: shard_body(): (weights[..., None] * gathered[..., :head_dim]).sum(axis=0)]
    slice x2 -> x0, other arithmetic: 11.9 us -> none  [shard_body(): total = (weights * gathered[..., head_dim + 1]).sum(axis=0)]
  transfers between devices with their start and end apart: 6 -> 0, of which waited for: 5 -> 0; matrix products, arithmetic and copies ran while one was open for 21% -> 0% of each run, Pallas kernels for 0% -> 0%
where the time goes in v1:
time: 125 us
  Pallas kernels  117 us (94%)
  local copies, waits for them, and re-layouts  5.12 us (4%)
  other arithmetic  2.03 us (2%)
    pallas_call x1, Pallas kernels, mlp(): pl.pallas_call(mlp_kernel, out_shape=jax.ShapeDtypeStruct(hidden.shape, B...  83.2 us
    pallas_call x1, Pallas kernels, attention(): pl.pallas_call(attn_kernel, out_shape=(jax.ShapeDtypeStruct((n_rows, widt...  33.6 us

profile of v1, /device:TPU:1, one launch (start us, length us, event | category | flops | bytes accessed | tf_op | source)
XLA Modules:
  0.0 124.6 jit_solution(10237865183738836336)
XLA Ops:
  0.6 0.7 add_convert_fusion
  1.3 0.1 convert_element_type.11
  1.4 1.3 %broadcast_in_dim.16.norm_ref = bf16[1,2560]{1,0:T(2,128)(2,1)} reshape(bf16[2560]{0:T(1024)(128)(2,1)} %param.26) | data formatting | bytes 10240 | tf_op jit(solution)/shard_map/broadcast_in_dim | solution.py:537
  2.7 1.3 %broadcast_in_dim.19.norm_ref = bf16[1,2560]{1,0:T(2,128)(2,1)} reshape(bf16[2560]{0:T(1024)(128)(2,1)} %param.27) | data formatting | bytes 10240 | tf_op jit(solution)/shard_map/broadcast_in_dim | solution.py:540
  4.0 0.5 fusion
  4.5 0.8 pad_maximum_fusion
  5.3 33.6 %attn.1 = (f32[256,1152]{1,0:T(8,128)}, bf16[64,512,128]{2,1,0:T(8,128)(2,1)}, bf16[64,512,128]{2,1,0:T(8,128)(2,1)}) custom-call(s32[64]{0:T(128)} %start_ref.1, bf16[256,2560]{1,0:T(8,128)(2,1)} %bitcast.10, f32[256,128]{1,0:T(8,128)} %get-tuple-element.12.cos_ref, f32[256,128]{1,0:T(8,128)} %get-tuple-element.13.sin_ref, ...), custom_call_target="tpu_custom_call" | custom-call | tf_op jit(solution)/shard_map/attn/pallas_call | solution.py:185
  38.9 83.2 %combine_mlp.1 = bf16[4,64,2560]{2,1,0:T(8,128)(2,1)} custom-call(f32[4,64,1152]{2,1,0:T(8,128)} %bitcast.11, bf16[4,64,2560]{2,1,0:T(8,128)(2,1)} %hid_ref.1, bf16[1,2560]{1,0:T(2,128)(2,1)} %broadcast_in_dim.19.norm_ref, bf16[1024,2560]{1,0:T(8,128)(2,1)} %wo_ref.1, bf16[2560,2432]{1,0:T(8,128)(2,1)} %wg_ref.1, bf16[2560,2432]{1,0:T(8,128)(2,1)} %wu_ref.1, ...), custom_call_target="tpu_custom_call" | custom-call | tf_op jit(solution)/shard_map/combine_mlp/pallas_call | solution.py:491
  122.1 2.5 %copy.19 = bf16[4,64,2560]{2,1,0:T(8,128)(2,1)} copy(bf16[4,64,2560]{2,1,0:T(8,128)(2,1)} %combine_mlp.1) | data formatting | bytes 2621440
  (1 shorter events, 0.0 us)

commit v2 on v1

--- a/solution.py
+++ b/solution.py
@@ -1,6 +1,7 @@
 import functools
 import jax
 import jax.numpy as jnp
+import numpy as np
 from jax import lax
 from jax.experimental import pallas as pl
 from jax.experimental.pallas import tpu as pltpu
@@ -13,9 +14,9 @@
 BF16 = jnp.bfloat16
 MESH = pl.DeviceIdType.MESH
 STATS = 128
-GROUP = 4
+GROUP = 8
 PIECE = 256
-LAG = 2
+LAG = 3
 VMEM_LIMIT = 66_900_000
 
 
@@ -23,9 +24,10 @@
     return jnp.dot(a, b, preferred_element_type=F32)
 
 
-def attn_kernel(start_ref, hid_ref, cos_ref, sin_ref, norm_ref, qg_ref, kg_ref, wq_ref, wk_ref, wv_ref, kc_ref, vc_ref,
+def attn_kernel(start_ref, hid_ref, freq_ref, norm_ref, qg_ref, kg_ref, wq_ref, wk_ref, wv_ref, kc_ref, vc_ref,
                 o_ref, ko_ref, vo_ref,
-                hid, normed, wq, wk, wv, kbuf, vbuf, qs, ks, vs, ostage, thr, hid_sem, w_sem, in_sem, out_sem, o_sem):
+                hid, normed, wq, wk, wv, kbuf, vbuf, cos, sin, raw, qs, ks, vs, ostage, thr, gain,
+                hid_sem, w_sem, in_sem, out_sem, o_sem):
     n_rows, d_model = hid.shape
     n_batch, rows_kv, hd = kbuf.shape
     n_steps = n_rows // n_batch
@@ -73,48 +75,76 @@
     row_kv = ri // (qrows // kv)
     thr[...] = jnp.where(ci % kv == row_kv, ci - kv * (ri % n_steps), 1 << 24)
 
+    def set_pos(b, c):
+        for i in range(n_steps):
+            cos[pl.ds(b * n_steps + i, 1), :] = jnp.full((1, hd), start_ref[b] + i, jnp.int32).astype(F32)
+        return c
+
+    lax.fori_loop(0, n_batch, set_pos, 0)
+    trows = 64
+    low = lax.broadcasted_iota(jnp.int32, (trows, hd), 1) < hd // 2
+
+    def table(i, c):
+        rows = pl.ds(pl.multiple_of(i * trows, trows), trows)
+        angle = cos[rows, :] * freq_ref[...]
+        s = jnp.sin(angle)
+        sin[rows, :] = jnp.where(low, -s, s)
+        cos[rows, :] = jnp.cos(angle)
+        return c
+
+    lax.fori_loop(0, n_rows // trows, table, 0)
+
+    for j in range(d_model // 128):
+        gain[:, j * 128:(j + 1) * 128] = jnp.broadcast_to(norm_ref[j:j + 1, :].astype(F32), (8, 128))
+
     hid_cp.wait()
-    gain = norm_ref[...].astype(F32)
-    chunk = 32
+    chunk = 16
 
     def norm_rows(i, c):
-        rows = pl.ds(pl.multiple_of(i * chunk, chunk), chunk)
-        x = hid[rows, :].astype(F32)
-        inv = lax.rsqrt(jnp.mean(x * x, axis=-1, keepdims=True) + NORM_EPS)
-        normed[rows, :] = (x * inv * gain).astype(BF16)
-        return c
-
-    lax.fori_loop(0, n_rows // chunk, norm_rows, 0)
+        for u in range(4):
+            rows = pl.ds(pl.multiple_of(i * 4 * chunk + u * chunk, chunk), chunk)
+            x = hid[rows, :].astype(F32)
+            inv = lax.rsqrt(jnp.mean(x * x, axis=-1, keepdims=True) + NORM_EPS)
+            x = x * inv
+            normed[rows, :] = jnp.concatenate([x[:8] * gain[...], x[8:] * gain[...]], axis=0).astype(BF16)
+        return c
+
+    lax.fori_loop(0, n_rows // (4 * chunk), norm_rows, 0)
 
     pi = lax.broadcasted_iota(jnp.int32, (n_rows, n_rows), 0)
     pj = lax.broadcasted_iota(jnp.int32, (n_rows, n_rows), 1)
     perm = jnp.where(pj == (pi % n_steps) * n_batch + pi // n_steps, 1.0, 0.0).astype(BF16)
-
-    def norm_rope(x, g):
+    for j in range(d_model // 256):
+        sl = slice(j * 256, (j + 1) * 256)
+        hid[:, sl] = dot(perm, normed[:, sl]).astype(BF16)
+
+    def norm_rope(x, g, rows):
         inv = lax.rsqrt(jnp.mean(x * x, axis=-1, keepdims=True) + NORM_EPS)
         x = x * inv * g
-        return x * cos_ref[...] + pltpu.roll(x, hd // 2, 1) * sin_ref[...]
+        return (x * cos[rows, :] + pltpu.roll(x, hd // 2, 1) * sin[rows, :]).astype(BF16).astype(F32)
 
     qg = qg_ref[...].astype(F32)
     kg = kg_ref[...].astype(F32)
-    for i in range(n_q + 2):
-        w_cps[i].wait()
-        if i < n_q:
-            raw = dot(normed[...], wq[:, i * 256:(i + 1) * 256])
-        elif i == n_q:
-            raw = dot(normed[...], wk[...])
-        else:
-            raw = dot(normed[...], wv[...])
-        if i <= n_q:
-            g = qg if i < n_q else kg
-            raw = jnp.concatenate([norm_rope(raw[:, :hd], g), norm_rope(raw[:, hd:], g)], axis=1)
-        done = dot(perm, raw.astype(BF16))
-        if i < n_q:
-            qs[:, i * 256:(i + 1) * 256] = done
-        elif i == n_q:
-            ks[...] = done
-        else:
-            vs[...] = done
+
+    def post(i):
+        for r in range(n_rows // 64):
+            rows = slice(r * 64, (r + 1) * 64)
+            for h in range(2):
+                x = raw[i % 2, rows, h * hd:(h + 1) * hd]
+                if i < n_q:
+                    qs[rows, i * 256 + h * hd:i * 256 + (h + 1) * hd] = norm_rope(x, qg, rows)
+                elif i == n_q:
+                    ks[rows, h * hd:(h + 1) * hd] = norm_rope(x, kg, rows)
+                else:
+                    vs[rows, h * hd:(h + 1) * hd] = x.astype(BF16).astype(F32)
+
+    for i in range(n_q + 3):
+        if i < n_q + 2:
+            w_cps[i].wait()
+            w = wq[:, i * 256:(i + 1) * 256] if i < n_q else (wk[...] if i == n_q else wv[...])
+            raw[i % 2] = dot(hid[...], w)
+        if i > 0:
+            post(i - 1)
 
     scale = hd ** -0.5
     grows = GROUP * n_steps
@@ -126,29 +156,35 @@
         cache_in(g, 1).wait()
         rows = pl.ds(pl.multiple_of(g * grows, grows), grows)
         q_slab = qs[rows, :]
-        k_slab = ks[rows, :]
-        v_slab = vs[rows, :]
-        outs, maxes, sums = [], [], []
+        offs = []
         for r in range(GROUP):
             b = g * GROUP + r
             off = kv * (start_ref[b] - blk_start)
+            offs.append(off)
             win = pl.multiple_of(jnp.clip((off // 16) * 16, 0, rows_kv - 32), 16)
-            for buf, slab in ((kbuf, k_slab), (vbuf, v_slab)):
+            for buf, new_ref in ((kbuf, ks), (vbuf, vs)):
+                slab = new_ref[rows, :]
                 cur = buf[b, pl.ds(win, 32), :].astype(F32)
                 for j in range(n_steps):
                     for h in range(kv):
                         new = slab[r * n_steps + j:r * n_steps + j + 1, h * hd:(h + 1) * hd]
                         cur = jnp.where(win_rows == off + kv * j + h - win, new, cur)
                 buf[b, pl.ds(win, 32), :] = cur.astype(BF16)
+        scores = []
+        for r in range(GROUP):
             q = jnp.concatenate([q_slab[r * n_steps:(r + 1) * n_steps, h * hd:(h + 1) * hd] for h in range(heads)], axis=0)
-            s = lax.dot_general(q.astype(BF16), kbuf[b], (((1,), (1,)), ((), ())), preferred_element_type=F32) * scale
-            keep = thr[...] <= off + kv - 1
-            s = jnp.where(keep, s, NEG)
+            scores.append(lax.dot_general(q.astype(BF16), kbuf[g * GROUP + r], (((1,), (1,)), ((), ())),
+                                          preferred_element_type=F32))
+        probs, maxes, sums = [], [], []
+        for r in range(GROUP):
+            keep = thr[...] <= offs[r] + kv - 1
+            s = jnp.where(keep, scores[r] * scale, NEG)
             m = jnp.max(s, axis=-1, keepdims=True)
             p = jnp.where(keep, jnp.exp(s - m), 0.0)
             sums.append(jnp.sum(p, axis=-1, keepdims=True))
             maxes.append(m)
-            outs.append(dot(p.astype(BF16), vbuf[b]))
+            probs.append(p.astype(BF16))
+        outs = [dot(probs[r], vbuf[g * GROUP + r]) for r in range(GROUP)]
         stats = jnp.zeros((grows, STATS), F32)
         for h in range(heads):
             sl = slice(h * n_steps, (h + 1) * n_steps)
@@ -172,7 +208,7 @@
     lax.fori_loop(0, n_groups, drain, 0)
 
 
-def attention(start_pos, hidden, cos, sin, attn_norm, q_gain, k_gain, w_q, w_k, w_v, k_cache, v_cache):
+def attention(start_pos, hidden, freq, attn_norm, q_gain, k_gain, w_q, w_k, w_v, k_cache, v_cache):
     n_rows, d_model = hidden.shape
     n_batch, rows_kv, hd = k_cache.shape
     heads = w_q.shape[1] // hd
@@ -186,22 +222,23 @@
         attn_kernel,
         out_shape=(jax.ShapeDtypeStruct((n_rows, width), F32),
                    jax.ShapeDtypeStruct(k_cache.shape, BF16), jax.ShapeDtypeStruct(v_cache.shape, BF16)),
-        in_specs=[pl.BlockSpec(memory_space=pltpu.SMEM), hbm, vmem, vmem, vmem, vmem, vmem, hbm, hbm, hbm, hbm, hbm],
+        in_specs=[pl.BlockSpec(memory_space=pltpu.SMEM), hbm, vmem, vmem, vmem, vmem, hbm, hbm, hbm, hbm, hbm],
         out_specs=(hbm, hbm, hbm),
         scratch_shapes=[
             pltpu.VMEM((n_rows, d_model), BF16), pltpu.VMEM((n_rows, d_model), BF16),
             pltpu.VMEM(w_q.shape, BF16), pltpu.VMEM(w_k.shape, BF16), pltpu.VMEM(w_v.shape, BF16),
             pltpu.VMEM(k_cache.shape, BF16), pltpu.VMEM(v_cache.shape, BF16),
+            pltpu.VMEM((n_rows, hd), F32), pltpu.VMEM((n_rows, hd), F32), pltpu.VMEM((2, n_rows, 256), F32),
             pltpu.VMEM((n_rows, w_q.shape[1]), F32), pltpu.VMEM((n_rows, w_k.shape[1]), F32),
             pltpu.VMEM((n_rows, w_v.shape[1]), F32), pltpu.VMEM((n_rows, width), F32),
-            pltpu.VMEM((heads * n_steps, rows_kv), jnp.int32),
+            pltpu.VMEM((heads * n_steps, rows_kv), jnp.int32), pltpu.VMEM((8, d_model), F32),
             pltpu.SemaphoreType.DMA, pltpu.SemaphoreType.DMA((n_w,)),
             pltpu.SemaphoreType.DMA((2, n_groups)), pltpu.SemaphoreType.DMA((2, n_groups)),
             pltpu.SemaphoreType.DMA((n_groups,)),
         ],
         compiler_params=pltpu.CompilerParams(vmem_limit_bytes=60_000_000),
         name="attn",
-    )(start_pos, hidden, cos, sin, attn_norm, q_gain, k_gain, w_q, w_k, w_v, k_cache, v_cache)
+    )(start_pos, hidden, freq, attn_norm, q_gain, k_gain, w_q, w_k, w_v, k_cache, v_cache)
 
 
 def mlp_kernel(o_ref, hid_ref, norm_ref, wo_ref, wg_ref, wu_ref, wd_ref,
@@ -388,8 +425,10 @@
     d_model = n_pieces * PIECE
     inv = lax.rsqrt(jnp.sum(sq, axis=-1, keepdims=True) * (1.0 / d_model) + NORM_EPS)
     for k in range(n_pieces):
-        g = norm_ref[:, k * PIECE:(k + 1) * PIECE].astype(F32)
-        mlp_in[:, k * PIECE:(k + 1) * PIECE] = (rbuf[k] * inv * g).astype(BF16)
+        for j in range(PIECE // 128):
+            c0 = k * PIECE + j * 128
+            g = norm_ref[c0 // 128:c0 // 128 + 1, :].astype(F32)
+            mlp_in[:, c0:c0 + 128] = (rbuf[k, :, j * 128:(j + 1) * 128] * inv * g).astype(BF16)
 
     w_cps[1].wait()
     w_cps[2].wait()
@@ -526,18 +565,14 @@
     def shard_body(hidden, start_pos, k_cache, v_cache, w_q, w_k, w_v, w_o, w_gate, w_up, w_down, attn_norm, mlp_norm, q_gain, k_gain):
         n_steps, n_batch, d_model = hidden.shape
         _, seq, kv, hd = k_cache.shape
-        half = hd // 2
-        freqs = ROPE_BASE ** (-(jnp.arange(half, dtype=F32) * (2.0 / hd)))
-        tok_pos = (start_pos[None, :] + jnp.arange(n_steps)[:, None]).reshape(-1)
-        angles = tok_pos.astype(F32)[:, None] * freqs[None, :]
-        cos, sin = jnp.cos(angles), jnp.sin(angles)
-        cos = jnp.concatenate([cos, cos], axis=1)
-        sin = jnp.concatenate([-sin, sin], axis=1)
+        half = np.arange(hd // 2)
+        freq = ROPE_BASE ** (-half * (2.0 / hd))
+        freq = jnp.asarray(np.concatenate([freq, freq])[None], F32)
         o_part, k_out, v_out = attention(
-            start_pos, hidden.reshape(-1, d_model), cos, sin, attn_norm[None], q_gain[None], k_gain[None],
+            start_pos, hidden.reshape(-1, d_model), freq, attn_norm.reshape(-1, 128), q_gain[None], k_gain[None],
             w_q, w_k, w_v, k_cache.reshape(n_batch, seq * kv, hd), v_cache.reshape(n_batch, seq * kv, hd))
         n_sp = 4
-        out = mlp(o_part.reshape(n_sp, -1, o_part.shape[1]), hidden, mlp_norm[None], w_o, w_gate, w_up, w_down)
+        out = mlp(o_part.reshape(n_sp, -1, o_part.shape[1]), hidden, mlp_norm.reshape(-1, 128), w_o, w_gate, w_up, w_down)
         return out, k_out.reshape(k_cache.shape), v_out.reshape(v_cache.shape)
 
     return jax.shard_map(shard_body, mesh=mesh, in_specs=in_specs, out_specs=out_specs, check_vma=False)

time: 125 us -> 104 us (0.83)
  Pallas kernels: 117 us -> 101 us
  local copies, waits for them, and re-layouts: 5.12 us -> 2.46 us
  other arithmetic: 2.03 us -> 0 us
    pallas_call x1, Pallas kernels: 33.6 us -> 19.6 us  [attention(): pl.pallas_call(attn_kernel, out_shape=(jax.ShapeDtypeStruct((n_rows, widt...]
    broadcast_in_dim x2 -> x0, local copies, waits for them, and re-layouts: 2.58 us -> none  [the longest x1 1.29 us: shard_body(): mlp_norm[None]]
    pallas_call x1, Pallas kernels: 83.2 us -> 81.4 us  [mlp(): pl.pallas_call(mlp_kernel, out_shape=jax.ShapeDtypeStruct(hidden.shape, B...]
where the time goes in v2:
time: 104 us
  Pallas kernels  101 us (97%)
  local copies, waits for them, and re-layouts  2.46 us (2%)
    pallas_call x1, Pallas kernels, mlp(): pl.pallas_call(mlp_kernel, out_shape=jax.ShapeDtypeStruct(hidden.shape, B...  81.4 us
    pallas_call x1, Pallas kernels, attention(): pl.pallas_call(attn_kernel, out_shape=(jax.ShapeDtypeStruct((n_rows, widt...  19.6 us
    unnamed x1, local copies, waits for them, and re-layouts  2.46 us

profile of v2, /device:TPU:1, one launch (start us, length us, event | category | flops | bytes accessed | tf_op | source)
XLA Modules:
  0.0 104.1 jit_solution(6281230333847015928)
XLA Ops:
  0.6 19.6 %attn.1 = (f32[256,1152]{1,0:T(8,128)}, bf16[64,512,128]{2,1,0:T(8,128)(2,1)}, bf16[64,512,128]{2,1,0:T(8,128)(2,1)}) custom-call(s32[64]{0:T(128)} %start_ref.1, bf16[256,2560]{1,0:T(8,128)(2,1)} %bitcast.12, f32[1,128]{1,0:T(1,128)} %constant.2.clone.freq_ref, bf16[20,128]{1,0:T(8,128)(2,1)} %bitcast.14, bf16[1,128]{1,0:T(2,128)(2,1)} %bitcast.16, ...), custom_call_target="tpu_custom_call" | custom-call | tf_op jit(solution)/shard_map/attn/pallas_call | solution.py:221
  20.3 81.4 %combine_mlp.1 = bf16[4,64,2560]{2,1,0:T(8,128)(2,1)} custom-call(f32[4,64,1152]{2,1,0:T(8,128)} %bitcast.13, bf16[4,64,2560]{2,1,0:T(8,128)(2,1)} %hid_ref.1, bf16[20,128]{1,0:T(8,128)(2,1)} %bitcast.15, bf16[1024,2560]{1,0:T(8,128)(2,1)} %wo_ref.1, bf16[2560,2432]{1,0:T(8,128)(2,1)} %wg_ref.1, bf16[2560,2432]{1,0:T(8,128)(2,1)} %wu_ref.1, ...), custom_call_target="tpu_custom_call" | custom-call | tf_op jit(solution)/shard_map/combine_mlp/pallas_call | solution.py:530
  101.7 2.5 %copy.20 = bf16[4,64,2560]{2,1,0:T(8,128)(2,1)} copy(bf16[4,64,2560]{2,1,0:T(8,128)(2,1)} %combine_mlp.1) | data formatting | bytes 2621440

commit v3 on v2

--- a/solution.py
+++ b/solution.py
@@ -16,7 +16,10 @@
 STATS = 128
 GROUP = 8
 PIECE = 256
-LAG = 3
+LAG = 5
+FLAG = 4
+GU_BLOCK = 384
+FLUSH = True
 VMEM_LIMIT = 66_900_000
 
 
@@ -257,7 +260,8 @@
     inner = jnp.logical_or(tp == 1, tp == 2)
     leaf = jnp.logical_or(tp == 0, tp == 3)
 
-    n_pieces, n_rows, _ = rbuf.shape
+    n_half, n_rows, d_model = x.shape
+    n_pieces = d_model // PIECE
     width = loc.shape[2]
     hd = 128
     heads = (width - STATS) // hd
@@ -265,20 +269,20 @@
     crows = dbuf.shape[2]
     n_steps = out_ref.shape[0]
     n_req = n_rows // n_steps
+    blk_req = n_req * n_half
 
     w_cps = [pltpu.make_async_copy(s, d, w_sem.at[i]) for i, (s, d) in
              enumerate(((wo_ref, wo), (wg_ref, wg), (wu_ref, wu), (wd_ref, wd)))]
     l_cps = [pltpu.make_async_copy(o_ref.at[oth], loc.at[0], l_sem.at[0]),
              pltpu.make_async_copy(o_ref.at[me], loc.at[1], l_sem.at[1])]
-    x_cps = [pltpu.make_async_copy(hid_ref.at[i, pl.ds(pl.multiple_of(me * n_req, n_req), n_req), :],
-                                   x.at[pl.ds(i * n_req, n_req), :], x_sem.at[i]) for i in range(n_steps)]
+    x_cps = [pltpu.make_async_copy(
+        hid_ref.at[i, pl.ds(pl.multiple_of(me * blk_req + h * n_req, n_req), n_req), :],
+        x.at[h, pl.ds(i * n_req, n_req), :], x_sem.at[h, i]) for h in range(n_half) for i in range(n_steps)]
     for cp in l_cps:
         cp.start()
     w_cps[0].start()
     for cp in x_cps:
         cp.start()
-    for cp in w_cps[1:]:
-        cp.start()
 
     barrier = pltpu.get_barrier_semaphore()
     for dev in ({'sp': mate}, {'sp': oth}, {'tp': side}):
@@ -311,187 +315,264 @@
 
     aw = heads * hd
 
-    def weights(sa, sb):
-        m = jnp.maximum(sa, sb)
-        ea = jnp.exp(sa - m)
-        eb = jnp.exp(sb - m)
-        tot = ea * pltpu.roll(sa, STATS - heads, 1) + eb * pltpu.roll(sb, STATS - heads, 1)
-        return m, ea, eb, tot
-
-    def pack_stats(m, tot):
-        lane = lax.broadcasted_iota(jnp.int32, m.shape, 1)
-        return jnp.where(lane < heads, m, pltpu.roll(tot, heads, 1))
-
-    def merge(a, ai, b, bi, dst, di):
-        m, ea, eb, tot = weights(a[ai + (slice(aw, None),)], b[bi + (slice(aw, None),)])
-        for h in range(heads):
-            sl = (slice(h * hd, (h + 1) * hd),)
-            dst[di + sl] = a[ai + sl] * ea[:, h:h + 1] + b[bi + sl] * eb[:, h:h + 1]
-        dst[di + (slice(aw, None),)] = pack_stats(m, tot)
-
+    def weights(parts):
+        m = functools.reduce(jnp.maximum, parts)
+        es = [jnp.exp(s - m) for s in parts]
+        tot = sum(e * pltpu.roll(s, STATS - heads, 1) for e, s in zip(es, parts))
+        return m, es, tot
+
+    stat_lane = lax.broadcasted_iota(jnp.int32, (crows, STATS), 1)
     l_cps[0].wait()
     for i in range(n_chunks):
         d_copy(0, i).wait_recv()
         rs = slice(i * crows, (i + 1) * crows)
-        merge(loc, (0, rs), dbuf, (0, i, slice(None)), ysend, (i, slice(None)))
+        m, (ea, eb), tot = weights((loc[0, rs, aw:], dbuf[0, i, :, aw:]))
+        for h in range(heads):
+            sl = slice(h * hd, (h + 1) * hd)
+            ysend[i, :, sl] = loc[0, rs, sl] * ea[:, h:h + 1] + dbuf[0, i, :, sl] * eb[:, h:h + 1]
+        ysend[i, :, aw:] = jnp.where(stat_lane < heads, m, pltpu.roll(tot, heads, 1))
         y_copy(i).start()
     l_cps[1].wait()
     for i in range(n_chunks):
         d_copy(1, i).wait_recv()
-        rs = slice(i * crows, (i + 1) * crows)
-        merge(loc, (1, rs), dbuf, (1, i, slice(None)), loc, (1, rs))
-    for i in range(n_chunks):
-        y_copy(i).wait_recv()
-        rs = slice(i * crows, (i + 1) * crows)
-        m, ea, eb, tot = weights(loc[1, rs, aw:], yrecv[i, :, aw:])
-        for h in range(heads):
-            sl = slice(h * hd, (h + 1) * hd)
-            val = loc[1, rs, sl] * ea[:, h:h + 1] + yrecv[i, :, sl] * eb[:, h:h + 1]
-            attn[rs, sl] = (val / tot[:, h:h + 1]).astype(BF16)
+    for cp in w_cps[1:]:
+        cp.start()
 
     pi = lax.broadcasted_iota(jnp.int32, (n_rows, n_rows), 0)
     pj = lax.broadcasted_iota(jnp.int32, (n_rows, n_rows), 1)
     perm = jnp.where(pj == (pi % n_req) * n_steps + pi // n_req, 1.0, 0.0).astype(BF16)
-    attn[...] = dot(perm, attn[...]).astype(BF16)
-
-    def up(a, k):
-        return remote(pbuf.at[a, k], in_leaf.at[a, k], up_s.at[a, k], up_r.at[a, k], {'tp': side})
-
-    def across(a, k):
-        return remote(pbuf.at[a, k], in_mid.at[a, k], mid_s.at[a, k], mid_r.at[a, k], {'tp': mid})
-
-    def down(a, k):
-        return remote(tbuf.at[a, k], tbuf.at[a, k], dn_s.at[a, k], dn_r.at[a, k], {'tp': side})
-
-    def all_reduce(a, part, finish):
+
+    def attn_half(hf):
+        per = n_chunks // n_half
+        for c in range(per):
+            i = hf * per + c
+            y_copy(i).wait_recv()
+            rs = slice(i * crows, (i + 1) * crows)
+            _, es, tot = weights((loc[1, rs, aw:], dbuf[1, i, :, aw:], yrecv[i, :, aw:]))
+            inv = 1.0 / tot
+            ea, eb, ec = [e * inv for e in es]
+            for h in range(heads):
+                sl = slice(h * hd, (h + 1) * hd)
+                val = (loc[1, rs, sl] * ea[:, h:h + 1] + dbuf[1, i, :, sl] * eb[:, h:h + 1]
+                       + yrecv[i, :, sl] * ec[:, h:h + 1])
+                attn[hf, c * crows:(c + 1) * crows, sl] = val.astype(BF16)
+        attn[hf] = dot(perm, attn[hf]).astype(BF16)
+
+    def up(a, u):
+        return remote(pbuf.at[a, u], in_leaf.at[a, u], up_s.at[a, u], up_r.at[a, u], {'tp': side})
+
+    def across(a, u):
+        return remote(pbuf.at[a, u], in_mid.at[a, u], mid_s.at[a, u], mid_r.at[a, u], {'tp': mid})
+
+    def down(a, u):
+        return remote(tbuf.at[a, u], tbuf.at[a, u], dn_s.at[a, u], dn_r.at[a, u], {'tp': side})
+
+    def cols(k):
+        if isinstance(k, int):
+            return pl.ds(k * PIECE, PIECE)
+        return pl.ds(pl.multiple_of(k * PIECE, PIECE), PIECE)
+
+    def part(a, hf, k):
+        left, right = ((attn, wo), (act, wd))[a]
+        pbuf[a, hf * n_pieces + k] = dot(left[hf], right[:, cols(k)])
+
+    def stage_a(a, u):
+        up(a, u).wait_recv()
+        pbuf[a, u] = pbuf[a, u] + in_leaf[a, u]
+        across(a, u).start()
+
+    def stage_b(a, u):
+        across(a, u).wait_recv()
+        tbuf[a, u] = pbuf[a, u] + in_mid[a, u]
+        down(a, u).start()
+        if a == 1:
+            finish_out(u)
+
+    def loop(lo, hi, body):
+        def step(k, c):
+            body(k)
+            return c
+        lax.fori_loop(lo, hi, step, 0)
+
+    def norm_half(hf):
+        base = hf * n_pieces
+
         @pl.when(leaf)
         def _():
-            def send(k, c):
-                pbuf[a, k] = part(k)
-                up(a, k).start()
-                return c
-            lax.fori_loop(0, n_pieces, send, 0)
-
-            def take(k, c):
-                down(a, k).wait_recv()
-                finish(k)
-                return c
-            lax.fori_loop(0, n_pieces, take, 0)
-
-        @pl.when(inner)
-        def _():
-            def stage_a(k):
-                mine = part(k)
-                up(a, k).wait_recv()
-                pbuf[a, k] = mine + in_leaf[a, k]
-                across(a, k).start()
-
-            def stage_b(k):
-                across(a, k).wait_recv()
-                tbuf[a, k] = pbuf[a, k] + in_mid[a, k]
-                down(a, k).start()
-                finish(k)
-
-            for k in range(LAG):
-                stage_a(k)
-
-            def body(k, c):
-                stage_a(k)
-                stage_b(k - LAG)
-                return c
-            lax.fori_loop(LAG, n_pieces, body, 0)
-            for k in range(n_pieces - LAG, n_pieces):
-                stage_b(k)
-
-    def cols(k):
-        return pl.ds(pl.multiple_of(k * PIECE, PIECE), PIECE)
+            loop(0, n_pieces, lambda k: down(0, base + k).wait_recv())
+        sq = jnp.zeros((n_rows, 128), F32)
+        for k in range(n_pieces):
+            r = (x[hf, :, cols(k)].astype(F32) + tbuf[0, base + k]).astype(BF16).astype(F32)
+            rbuf[base + k] = r
+            for j in range(PIECE // 128):
+                piece = r[:, j * 128:(j + 1) * 128]
+                sq = sq + piece * piece
+        inv = lax.rsqrt(jnp.sum(sq, axis=-1, keepdims=True) * (1.0 / d_model) + NORM_EPS)
+        for k in range(n_pieces):
+            for j in range(PIECE // 128):
+                c0 = k * PIECE + j * 128
+                g = norm_ref[c0 // 128:c0 // 128 + 1, :].astype(F32)
+                mlp_in[hf, :, c0:c0 + 128] = (rbuf[base + k, :, j * 128:(j + 1) * 128] * inv * g).astype(BF16)
+
+    ffn = wg.shape[1]
+    blocks = [(c, min(GU_BLOCK, ffn - c)) for c in range(0, ffn, GU_BLOCK)]
+    def gate_up(hf, serve):
+        for j, (c0, size) in enumerate(blocks):
+            sl = slice(c0, c0 + size)
+            gate = dot(mlp_in[hf], wg[:, sl])
+            upv = dot(mlp_in[hf], wu[:, sl])
+            act[hf, :, sl] = (gate * (1.0 / (1.0 + jnp.exp(-gate))) * upv).astype(BF16)
+
+            late = range(j * LAG // len(blocks), (j + 1) * LAG // len(blocks))
+            if len(late):
+                @pl.when(inner)
+                def _():
+                    for i in late:
+                        serve(i)
+
+    def put(blk, hf, k, val):
+        val = val.astype(BF16)
+        for i in range(n_steps):
+            out_ref[i, pl.ds(pl.multiple_of(blk * blk_req + hf * n_req, n_req), n_req), cols(k)] = val[i * n_req:(i + 1) * n_req]
+
+    def f_y(u):
+        return remote(fbuf.at[u], fy.at[u], fy_s.at[u], fy_r.at[u], {'sp': oth})
+
+    def f_d(which, u):
+        src = (fbuf, fy)[which]
+        return remote(src.at[u], fd.at[which, u], fd_s.at[which, u], fd_r.at[which, u], {'sp': mate})
+
+    def forward(u):
+        f_y(u).wait_recv()
+        f_d(1, u).start()
+        put(oth, u // n_pieces, u % n_pieces, fy[u])
+
+    def finish_out(u):
+        val = (rbuf[u] + tbuf[1, u]).astype(BF16)
+        fbuf[u] = val.astype(F32)
+        f_y(u).start()
+        f_d(0, u).start()
+        put(me, u // n_pieces, u % n_pieces, val)
+        if isinstance(u, int):
+            if u >= FLAG:
+                forward(u - FLAG)
+        else:
+            @pl.when(u >= FLAG)
+            def _():
+                forward(u - FLAG)
 
     w_cps[0].wait()
+    attn_half(0)
+
+    @pl.when(leaf)
+    def _():
+        def body(k):
+            part(0, 0, k)
+            up(0, k).start()
+        loop(0, n_pieces, body)
+
+    @pl.when(inner)
+    def _():
+        def head(k):
+            part(0, 0, k)
+            stage_a(0, k)
+        loop(0, LAG, head)
+
+        def body(k):
+            head(k)
+            stage_b(0, k - LAG)
+        loop(LAG, n_pieces, body)
+        if FLUSH:
+            loop(n_pieces - LAG, n_pieces, lambda u: stage_b(0, u))
+
+    attn_half(1)
+
+    @pl.when(leaf)
+    def _():
+        def body(k):
+            part(0, 1, k)
+            up(0, n_pieces + k).start()
+        loop(0, n_pieces, body)
+
+    @pl.when(inner)
+    def _():
+        def head(k):
+            part(0, 1, k)
+            stage_a(0, n_pieces + k)
+
+        def body(k):
+            head(k)
+            stage_b(0, n_pieces - LAG + k)
+        loop(0, LAG, head if FLUSH else body)
+        loop(LAG, n_pieces, body)
+
     for cp in x_cps:
         cp.wait()
-
-    def take_r(k):
-        r = (x[:, cols(k)].astype(F32) + tbuf[0, k]).astype(BF16).astype(F32)
-        rbuf[k] = r
-
-    all_reduce(0, lambda k: dot(attn[...], wo[:, cols(k)]), take_r)
-
-    sq = jnp.zeros((n_rows, 128), F32)
-    for k in range(n_pieces):
-        r = rbuf[k]
-        for j in range(PIECE // 128):
-            piece = r[:, j * 128:(j + 1) * 128]
-            sq = sq + piece * piece
-    d_model = n_pieces * PIECE
-    inv = lax.rsqrt(jnp.sum(sq, axis=-1, keepdims=True) * (1.0 / d_model) + NORM_EPS)
-    for k in range(n_pieces):
-        for j in range(PIECE // 128):
-            c0 = k * PIECE + j * 128
-            g = norm_ref[c0 // 128:c0 // 128 + 1, :].astype(F32)
-            mlp_in[:, c0:c0 + 128] = (rbuf[k, :, j * 128:(j + 1) * 128] * inv * g).astype(BF16)
-
+    norm_half(0)
     w_cps[1].wait()
     w_cps[2].wait()
-    ffn = wg.shape[1]
-    wide = 256
-
-    def gate_up(sl):
-        gate = dot(mlp_in[...], wg[:, sl])
-        upv = dot(mlp_in[...], wu[:, sl])
-        act[:, sl] = (gate * (1.0 / (1.0 + jnp.exp(-gate))) * upv).astype(BF16)
-
-    def gu_body(j, c):
-        gate_up(pl.ds(pl.multiple_of(j * wide, wide), wide))
-        return c
-    lax.fori_loop(0, ffn // wide, gu_body, 0)
-    if ffn % wide:
-        gate_up(pl.ds(ffn // wide * wide, ffn % wide))
-
+
+    gate_up(0, lambda j: stage_b(0, 2 * n_pieces - LAG + j))
     w_cps[3].wait()
 
-    def put(blk, k, val):
-        val = val.astype(BF16)
-        for i in range(n_steps):
-            out_ref[i, pl.ds(pl.multiple_of(blk * n_req, n_req), n_req), cols(k)] = val[i * n_req:(i + 1) * n_req]
-
-    def f_y(k):
-        return remote(fbuf.at[k], fy.at[k], fy_s.at[k], fy_r.at[k], {'sp': oth})
-
-    def f_d(which, k):
-        src = (fbuf, fy)[which]
-        return remote(src.at[k], fd.at[which, k], fd_s.at[which, k], fd_r.at[which, k], {'sp': mate})
-
-    def forward(k):
-        f_y(k).wait_recv()
-        f_d(1, k).start()
-        put(oth, k, fy[k])
-
-    def finish_out(k):
-        val = (rbuf[k] + tbuf[1, k]).astype(BF16)
-        fbuf[k] = val.astype(F32)
-        f_y(k).start()
-        f_d(0, k).start()
-        put(me, k, val)
-
-        if isinstance(k, int):
-            if k >= LAG:
-                forward(k - LAG)
-        else:
-            @pl.when(k >= LAG)
-            def _():
-                forward(k - LAG)
-
-    all_reduce(1, lambda k: dot(act[...], wd[:, cols(k)]), finish_out)
-    for k in range(n_pieces - LAG, n_pieces):
-        forward(k)
-
-    def last(k, c):
-        f_d(0, k).wait_recv()
-        put(mate, k, fd[0, k])
-        f_d(1, k).wait_recv()
-        put(mate_oth, k, fd[1, k])
-        return c
-    lax.fori_loop(0, n_pieces, last, 0)
+    @pl.when(leaf)
+    def _():
+        def body(k):
+            part(1, 0, k)
+            up(1, k).start()
+        loop(0, n_pieces, body)
+
+    @pl.when(inner)
+    def _():
+        def head(k):
+            part(1, 0, k)
+            stage_a(1, k)
+        loop(0, LAG, head)
+
+        def body(k):
+            head(k)
+            stage_b(1, k - LAG)
+        loop(LAG, n_pieces, body)
+
+    norm_half(1)
+
+    gate_up(1, lambda j: stage_b(1, n_pieces - LAG + j))
+
+    @pl.when(leaf)
+    def _():
+        def body(k):
+            part(1, 1, k)
+            up(1, n_pieces + k).start()
+        loop(0, n_pieces, body)
+
+        def tail(u):
+            down(1, u).wait_recv()
+            finish_out(u)
+        loop(0, 2 * n_pieces, tail)
+
+    @pl.when(inner)
+    def _():
+        def head(k):
+            part(1, 1, k)
+            stage_a(1, n_pieces + k)
+        loop(0, LAG, head)
+
+        def body(k):
+            head(k)
+            stage_b(1, n_pieces + k - LAG)
+        loop(LAG, n_pieces, body)
+        loop(2 * n_pieces - LAG, 2 * n_pieces, lambda u: stage_b(1, u))
+
+    loop(2 * n_pieces - FLAG, 2 * n_pieces, forward)
+
+    for hf in range(n_half):
+        def last(k, hf=hf):
+            u = hf * n_pieces + k
+            f_d(0, u).wait_recv()
+            put(mate, hf, k, fd[0, u])
+            f_d(1, u).wait_recv()
+            put(mate_oth, hf, k, fd[1, u])
+        loop(0, n_pieces, last)
 
     for which in range(2):
         for i in range(n_chunks):
@@ -499,55 +580,56 @@
     for i in range(n_chunks):
         y_copy(i).wait_send()
 
-    def sends(k, c):
-        f_y(k).wait_send()
-        f_d(0, k).wait_send()
-        f_d(1, k).wait_send()
+    def sends(u):
+        f_y(u).wait_send()
+        f_d(0, u).wait_send()
+        f_d(1, u).wait_send()
         for a in range(2):
             @pl.when(leaf)
             def _():
-                up(a, k).wait_send()
+                up(a, u).wait_send()
 
             @pl.when(inner)
             def _():
-                across(a, k).wait_send()
-                down(a, k).wait_send()
-        return c
-    lax.fori_loop(0, n_pieces, sends, 0)
+                across(a, u).wait_send()
+                down(a, u).wait_send()
+    loop(0, n_half * n_pieces, sends)
 
 
 def mlp(o_part, hidden, mlp_norm, w_o, w_gate, w_up, w_down):
-    n_blk, n_rows, width = o_part.shape
+    n_blk, blk_rows, width = o_part.shape
     n_steps, n_batch, d_model = hidden.shape
+    n_half = 2
+    n_rows = blk_rows // n_half
     n_pieces = d_model // PIECE
     n_chunks = 4
-    crows = n_rows // n_chunks
+    crows = blk_rows // n_chunks
     ffn = w_gate.shape[1]
     vmem = pl.BlockSpec(memory_space=pltpu.VMEM)
     hbm = pl.BlockSpec(memory_space=pl.ANY)
     dma = pltpu.SemaphoreType.DMA
-    piece = (n_pieces, n_rows, PIECE)
+    n_u = n_half * n_pieces
+    piece = (n_u, n_rows, PIECE)
     return pl.pallas_call(
         mlp_kernel,
         out_shape=jax.ShapeDtypeStruct(hidden.shape, BF16),
         in_specs=[hbm, hbm, vmem, hbm, hbm, hbm, hbm],
         out_specs=vmem,
         scratch_shapes=[
-            pltpu.VMEM((n_rows, d_model), BF16),
+            pltpu.VMEM((n_half, n_rows, d_model), BF16),
             pltpu.VMEM(w_o.shape, BF16), pltpu.VMEM(w_gate.shape, BF16),
             pltpu.VMEM(w_up.shape, BF16), pltpu.VMEM(w_down.shape, BF16),
-            pltpu.VMEM((2, n_rows, width), F32), pltpu.VMEM((2, n_chunks, crows, width), F32),
+            pltpu.VMEM((2, blk_rows, width), F32), pltpu.VMEM((2, n_chunks, crows, width), F32),
             pltpu.VMEM((n_chunks, crows, width), F32), pltpu.VMEM((n_chunks, crows, width), F32),
-            pltpu.VMEM((n_rows, w_o.shape[0]), BF16),
+            pltpu.VMEM((n_half, n_rows, w_o.shape[0]), BF16),
             pltpu.VMEM((2,) + piece, F32), pltpu.VMEM((2,) + piece, F32),
             pltpu.VMEM((2,) + piece, F32), pltpu.VMEM((2,) + piece, F32),
-            pltpu.VMEM(piece, F32), pltpu.VMEM((n_rows, d_model), BF16), pltpu.VMEM((n_rows, ffn), BF16),
+            pltpu.VMEM(piece, F32), pltpu.VMEM((n_half, n_rows, d_model), BF16), pltpu.VMEM((n_half, n_rows, ffn), BF16),
             pltpu.VMEM(piece, F32), pltpu.VMEM(piece, F32), pltpu.VMEM((2,) + piece, F32),
-            dma((n_steps,)), dma((4,)), dma((2,)),
+            dma((n_half, n_steps)), dma((4,)), dma((2,)),
             dma((2, n_chunks)), dma((2, n_chunks)), dma((n_chunks,)), dma((n_chunks,)),
-            dma((2, n_pieces)), dma((2, n_pieces)), dma((2, n_pieces)), dma((2, n_pieces)),
-            dma((2, n_pieces)), dma((2, n_pieces)),
-            dma((n_pieces,)), dma((n_pieces,)), dma((2, n_pieces)), dma((2, n_pieces)),
+            dma((2, n_u)), dma((2, n_u)), dma((2, n_u)), dma((2, n_u)), dma((2, n_u)), dma((2, n_u)),
+            dma((n_u,)), dma((n_u,)), dma((2, n_u)), dma((2, n_u)),
         ],
         compiler_params=pltpu.CompilerParams(vmem_limit_bytes=VMEM_LIMIT, collective_id=0, has_side_effects=True),
         name="combine_mlp",

time: 104 us -> 90.4 us (0.87)
  Pallas kernels: 101 us -> 87 us
    pallas_call x1, Pallas kernels: 81.4 us -> 67.4 us  [mlp(): pl.pallas_call(mlp_kernel, out_shape=jax.ShapeDtypeStruct(hidden.shape, B...]
where the time goes in v3:
time: 90.4 us; the launch traced here: 90.1 us
  Pallas kernels  87 us (96%)
  local copies, waits for them, and re-layouts  2.46 us (3%)
    pallas_call x1, Pallas kernels, mlp(): pl.pallas_call(mlp_kernel, out_shape=jax.ShapeDtypeStruct(hidden.shape, B...  67.4 us
    pallas_call x1, Pallas kernels, attention(): pl.pallas_call(attn_kernel, out_shape=(jax.ShapeDtypeStruct((n_rows, widt...  19.6 us
    unnamed x1, local copies, waits for them, and re-layouts  2.46 us

profile of v3, /device:TPU:1, one launch (start us, length us, event | category | flops | bytes accessed | tf_op | source)
XLA Modules:
  0.0 90.1 jit_solution(8650409352955862475)
XLA Ops:
  0.6 19.6 %attn.1 = (f32[256,1152]{1,0:T(8,128)}, bf16[64,512,128]{2,1,0:T(8,128)(2,1)}, bf16[64,512,128]{2,1,0:T(8,128)(2,1)}) custom-call(s32[64]{0:T(128)} %start_ref.1, bf16[256,2560]{1,0:T(8,128)(2,1)} %bitcast.12, f32[1,128]{1,0:T(1,128)} %constant.2.clone.freq_ref, bf16[20,128]{1,0:T(8,128)(2,1)} %bitcast.14, bf16[1,128]{1,0:T(2,128)(2,1)} %bitcast.16, ...), custom_call_target="tpu_custom_call" | custom-call | tf_op jit(solution)/shard_map/attn/pallas_call | solution.py:224
  20.3 67.4 %combine_mlp.1 = bf16[4,64,2560]{2,1,0:T(8,128)(2,1)} custom-call(f32[4,64,1152]{2,1,0:T(8,128)} %bitcast.13, bf16[4,64,2560]{2,1,0:T(8,128)(2,1)} %hid_ref.1, bf16[20,128]{1,0:T(8,128)(2,1)} %bitcast.15, bf16[1024,2560]{1,0:T(8,128)(2,1)} %wo_ref.1, bf16[2560,2432]{1,0:T(8,128)(2,1)} %wg_ref.1, bf16[2560,2432]{1,0:T(8,128)(2,1)} %wu_ref.1, ...), custom_call_target="tpu_custom_call" | custom-call | tf_op jit(solution)/shard_map/combine_mlp/pallas_call | solution.py:613
  87.7 2.5 %copy.20 = bf16[4,64,2560]{2,1,0:T(8,128)(2,1)} copy(bf16[4,64,2560]{2,1,0:T(8,128)(2,1)} %combine_mlp.1) | data formatting | bytes 2621440

commit v4 on v3

--- a/solution.py
+++ b/solution.py
@@ -9,17 +9,18 @@
 
 ROPE_BASE = 1000000.0
 NORM_EPS = 1e-06
-NEG = -3.0e38
+LOWEST = float(np.finfo(np.float32).min)
+LOG2E = 1.4426950408889634
 F32 = jnp.float32
 BF16 = jnp.bfloat16
 MESH = pl.DeviceIdType.MESH
 STATS = 128
 GROUP = 8
 PIECE = 256
-LAG = 5
+LAG = 4
 FLAG = 4
 GU_BLOCK = 384
-FLUSH = True
+PAIR = 2
 VMEM_LIMIT = 66_900_000
 
 
@@ -49,8 +50,7 @@
         w_cps.append(pltpu.make_async_copy(wq_ref.at[:, pl.ds(i * 256, 256)], wq.at[:, pl.ds(i * 256, 256)], w_sem.at[i]))
     w_cps.append(pltpu.make_async_copy(wk_ref, wk, w_sem.at[n_q]))
     w_cps.append(pltpu.make_async_copy(wv_ref, wv, w_sem.at[n_q + 1]))
-    for cp in w_cps:
-        cp.start()
+    w_cps[0].start()
 
     def cache_in(g, which):
         src, dst = ((kc_ref, kbuf), (vc_ref, vbuf))[which]
@@ -70,8 +70,6 @@
         cache_in(g, 0).start()
         cache_in(g, 1).start()
         return c
-
-    lax.fori_loop(0, n_groups, start_in, 0)
 
     ri = lax.broadcasted_iota(jnp.int32, (qrows, rows_kv), 0)
     ci = lax.broadcasted_iota(jnp.int32, (qrows, rows_kv), 1)
@@ -101,15 +99,22 @@
         gain[:, j * 128:(j + 1) * 128] = jnp.broadcast_to(norm_ref[j:j + 1, :].astype(F32), (8, 128))
 
     hid_cp.wait()
+    for cp in w_cps[1:]:
+        cp.start()
     chunk = 16
 
     def norm_rows(i, c):
         for u in range(4):
             rows = pl.ds(pl.multiple_of(i * 4 * chunk + u * chunk, chunk), chunk)
-            x = hid[rows, :].astype(F32)
-            inv = lax.rsqrt(jnp.mean(x * x, axis=-1, keepdims=True) + NORM_EPS)
-            x = x * inv
-            normed[rows, :] = jnp.concatenate([x[:8] * gain[...], x[8:] * gain[...]], axis=0).astype(BF16)
+            sq = jnp.zeros((chunk, 128), F32)
+            for j in range(d_model // 128):
+                x = hid[rows, j * 128:(j + 1) * 128].astype(F32)
+                sq = sq + x * x
+            inv = lax.rsqrt(jnp.sum(sq, axis=-1, keepdims=True) * (1.0 / d_model) + NORM_EPS)
+            for j in range(d_model // 128):
+                sl = slice(j * 128, (j + 1) * 128)
+                x = hid[rows, sl].astype(F32) * inv
+                normed[rows, sl] = jnp.concatenate([x[:8] * gain[:, sl], x[8:] * gain[:, sl]], axis=0).astype(BF16)
         return c
 
     lax.fori_loop(0, n_rows // (4 * chunk), norm_rows, 0)
@@ -137,15 +142,19 @@
                 if i < n_q:
                     qs[rows, i * 256 + h * hd:i * 256 + (h + 1) * hd] = norm_rope(x, qg, rows)
                 elif i == n_q:
-                    ks[rows, h * hd:(h + 1) * hd] = norm_rope(x, kg, rows)
+                    ks[pl.ds(r * 64 * kv + h, 64, stride=kv), :] = norm_rope(x, kg, rows)
                 else:
-                    vs[rows, h * hd:(h + 1) * hd] = x.astype(BF16).astype(F32)
+                    vs[pl.ds(r * 64 * kv + h, 64, stride=kv), :] = x.astype(BF16).astype(F32)
 
     for i in range(n_q + 3):
         if i < n_q + 2:
             w_cps[i].wait()
+            for g in range(n_groups * i // (n_q + 2), n_groups * (i + 1) // (n_q + 2)):
+                start_in(g, 0)
             w = wq[:, i * 256:(i + 1) * 256] if i < n_q else (wk[...] if i == n_q else wv[...])
-            raw[i % 2] = dot(hid[...], w)
+            for r in range(2):
+                rr = slice(r * n_rows // 2, (r + 1) * n_rows // 2)
+                raw[i % 2, rr] = dot(hid[rr], w)
         if i > 0:
             post(i - 1)
 
@@ -165,13 +174,13 @@
             off = kv * (start_ref[b] - blk_start)
             offs.append(off)
             win = pl.multiple_of(jnp.clip((off // 16) * 16, 0, rows_kv - 32), 16)
+            n_new = n_steps * kv
+            at = win_rows + (win - off)
+            hit = jnp.logical_and(at >= 0, at < n_new)
             for buf, new_ref in ((kbuf, ks), (vbuf, vs)):
-                slab = new_ref[rows, :]
+                new = pltpu.roll(new_ref[pl.ds(pl.multiple_of(b * n_new, n_new), n_new), :], off % n_new, 0)
                 cur = buf[b, pl.ds(win, 32), :].astype(F32)
-                for j in range(n_steps):
-                    for h in range(kv):
-                        new = slab[r * n_steps + j:r * n_steps + j + 1, h * hd:(h + 1) * hd]
-                        cur = jnp.where(win_rows == off + kv * j + h - win, new, cur)
+                cur = jnp.where(hit, jnp.concatenate([new] * (32 // n_new), axis=0), cur)
                 buf[b, pl.ds(win, 32), :] = cur.astype(BF16)
         scores = []
         for r in range(GROUP):
@@ -180,12 +189,11 @@
                                           preferred_element_type=F32))
         probs, maxes, sums = [], [], []
         for r in range(GROUP):
-            keep = thr[...] <= offs[r] + kv - 1
-            s = jnp.where(keep, scores[r] * scale, NEG)
-            m = jnp.max(s, axis=-1, keepdims=True)
-            p = jnp.where(keep, jnp.exp(s - m), 0.0)
+            s = jnp.where(thr[...] <= offs[r] + kv - 1, scores[r], -jnp.inf)
+            m = jnp.maximum(jnp.max(s, axis=-1, keepdims=True), LOWEST)
+            p = jnp.exp2((s - m) * (scale * LOG2E))
             sums.append(jnp.sum(p, axis=-1, keepdims=True))
-            maxes.append(m)
+            maxes.append(m * scale)
             probs.append(p.astype(BF16))
         outs = [dot(probs[r], vbuf[g * GROUP + r]) for r in range(GROUP)]
         stats = jnp.zeros((grows, STATS), F32)
@@ -232,8 +240,8 @@
             pltpu.VMEM(w_q.shape, BF16), pltpu.VMEM(w_k.shape, BF16), pltpu.VMEM(w_v.shape, BF16),
             pltpu.VMEM(k_cache.shape, BF16), pltpu.VMEM(v_cache.shape, BF16),
             pltpu.VMEM((n_rows, hd), F32), pltpu.VMEM((n_rows, hd), F32), pltpu.VMEM((2, n_rows, 256), F32),
-            pltpu.VMEM((n_rows, w_q.shape[1]), F32), pltpu.VMEM((n_rows, w_k.shape[1]), F32),
-            pltpu.VMEM((n_rows, w_v.shape[1]), F32), pltpu.VMEM((n_rows, width), F32),
+            pltpu.VMEM((n_rows, w_q.shape[1]), F32), pltpu.VMEM((n_rows * w_k.shape[1] // hd, hd), F32),
+            pltpu.VMEM((n_rows * w_v.shape[1] // hd, hd), F32), pltpu.VMEM((n_rows, width), F32),
             pltpu.VMEM((heads * n_steps, rows_kv), jnp.int32), pltpu.VMEM((8, d_model), F32),
             pltpu.SemaphoreType.DMA, pltpu.SemaphoreType.DMA((n_w,)),
             pltpu.SemaphoreType.DMA((2, n_groups)), pltpu.SemaphoreType.DMA((2, n_groups)),
@@ -280,9 +288,6 @@
         x.at[h, pl.ds(i * n_req, n_req), :], x_sem.at[h, i]) for h in range(n_half) for i in range(n_steps)]
     for cp in l_cps:
         cp.start()
-    w_cps[0].start()
-    for cp in x_cps:
-        cp.start()
 
     barrier = pltpu.get_barrier_semaphore()
     for dev in ({'sp': mate}, {'sp': oth}, {'tp': side}):
@@ -332,6 +337,10 @@
             ysend[i, :, sl] = loc[0, rs, sl] * ea[:, h:h + 1] + dbuf[0, i, :, sl] * eb[:, h:h + 1]
         ysend[i, :, aw:] = jnp.where(stat_lane < heads, m, pltpu.roll(tot, heads, 1))
         y_copy(i).start()
+        if i == 0:
+            w_cps[0].start()
+            for cp in x_cps:
+                cp.start()
     l_cps[1].wait()
     for i in range(n_chunks):
         d_copy(1, i).wait_recv()
@@ -393,6 +402,17 @@
             body(k)
             return c
         lax.fori_loop(lo, hi, step, 0)
+
+    def parts(a, hf):
+        def body(i):
+            for k in range(PAIR):
+                part(a, hf, i * PAIR + k)
+
+            @pl.when(leaf)
+            def _():
+                for k in range(PAIR):
+                    up(a, hf * n_pieces + i * PAIR + k).start()
+        loop(0, n_pieces // PAIR, body)
 
     def norm_half(hf):
         base = hf * n_pieces
@@ -423,12 +443,9 @@
             upv = dot(mlp_in[hf], wu[:, sl])
             act[hf, :, sl] = (gate * (1.0 / (1.0 + jnp.exp(-gate))) * upv).astype(BF16)
 
-            late = range(j * LAG // len(blocks), (j + 1) * LAG // len(blocks))
-            if len(late):
-                @pl.when(inner)
-                def _():
-                    for i in late:
-                        serve(i)
+            @pl.when(inner)
+            def _():
+                serve(j)
 
     def put(blk, hf, k, val):
         val = val.astype(BF16)
@@ -463,48 +480,30 @@
 
     w_cps[0].wait()
     attn_half(0)
+    parts(0, 0)
+    attn_half(1)
+    n_u = n_half * n_pieces
 
     @pl.when(leaf)
     def _():
-        def body(k):
-            part(0, 0, k)
-            up(0, k).start()
-        loop(0, n_pieces, body)
+        parts(0, 1)
 
     @pl.when(inner)
     def _():
-        def head(k):
-            part(0, 0, k)
-            stage_a(0, k)
+        def head(u):
+            part(0, 1, u)
+            stage_a(0, u)
         loop(0, LAG, head)
 
-        def body(k):
-            head(k)
-            stage_b(0, k - LAG)
+        def body(u):
+            head(u)
+            stage_b(0, u - LAG)
         loop(LAG, n_pieces, body)
-        if FLUSH:
-            loop(n_pieces - LAG, n_pieces, lambda u: stage_b(0, u))
-
-    attn_half(1)
-
-    @pl.when(leaf)
-    def _():
-        def body(k):
-            part(0, 1, k)
-            up(0, n_pieces + k).start()
-        loop(0, n_pieces, body)
-
-    @pl.when(inner)
-    def _():
-        def head(k):
-            part(0, 1, k)
-            stage_a(0, n_pieces + k)
-
-        def body(k):
-            head(k)
-            stage_b(0, n_pieces - LAG + k)
-        loop(0, LAG, head if FLUSH else body)
-        loop(LAG, n_pieces, body)
+
+        def rest(u):
+            stage_a(0, u)
+            stage_b(0, u - LAG)
+        loop(n_pieces, n_u, rest)
 
     for cp in x_cps:
         cp.wait()
@@ -512,56 +511,41 @@
     w_cps[1].wait()
     w_cps[2].wait()
 
-    gate_up(0, lambda j: stage_b(0, 2 * n_pieces - LAG + j))
+    def serve0(j):
+        if j < LAG:
+            stage_b(0, n_u - LAG + j)
+    gate_up(0, serve0)
     w_cps[3].wait()
+
+    parts(1, 0)
+    norm_half(1)
+    shares = [[int(u) for u in s] for s in np.array_split(np.arange(n_pieces), len(blocks))]
+
+    def serve1(j):
+        for u in shares[j]:
+            stage_a(1, u)
+            if u >= LAG:
+                stage_b(1, u - LAG)
+    gate_up(1, serve1)
+    parts(1, 1)
 
     @pl.when(leaf)
     def _():
-        def body(k):
-            part(1, 0, k)
-            up(1, k).start()
-        loop(0, n_pieces, body)
+        def take(u):
+            down(1, u).wait_recv()
+            finish_out(u)
+        loop(0, n_u, take)
 
     @pl.when(inner)
     def _():
-        def head(k):
-            part(1, 0, k)
-            stage_a(1, k)
-        loop(0, LAG, head)
-
-        def body(k):
-            head(k)
-            stage_b(1, k - LAG)
-        loop(LAG, n_pieces, body)
-
-    norm_half(1)
-
-    gate_up(1, lambda j: stage_b(1, n_pieces - LAG + j))
-
-    @pl.when(leaf)
-    def _():
-        def body(k):
-            part(1, 1, k)
-            up(1, n_pieces + k).start()
-        loop(0, n_pieces, body)
-
-        def tail(u):
-            down(1, u).wait_recv()
-            finish_out(u)
-        loop(0, 2 * n_pieces, tail)
-
-    @pl.when(inner)
-    def _():
-        def head(k):
-            part(1, 1, k)
-            stage_a(1, n_pieces + k)
-        loop(0, LAG, head)
-
-        def body(k):
-            head(k)
-            stage_b(1, n_pieces + k - LAG)
-        loop(LAG, n_pieces, body)
-        loop(2 * n_pieces - LAG, 2 * n_pieces, lambda u: stage_b(1, u))
+        loop(n_pieces - LAG, n_pieces, lambda u: stage_b(1, u))
+        loop(n_pieces, n_pieces + LAG, lambda u: stage_a(1, u))
+
+        def body(u):
+            stage_a(1, u)
+            stage_b(1, u - LAG)
+        loop(n_pieces + LAG, n_u, body)
+        loop(n_u - LAG, n_u, lambda u: stage_b(1, u))
 
     loop(2 * n_pieces - FLAG, 2 * n_pieces, forward)
 

time: 90.4 us -> 87.1 us (0.963)
  Pallas kernels: 87 us -> 83.7 us
    pallas_call x1, Pallas kernels: 19.6 us -> 15.9 us  [attention(): pl.pallas_call(attn_kernel, out_shape=(jax.ShapeDtypeStruct((n_rows, widt...]
where the time goes in v4:
time: 87.1 us; the launch traced here: 86.8 us
  Pallas kernels  83.7 us (96%)
  local copies, waits for them, and re-layouts  2.46 us (3%)
    pallas_call x1, Pallas kernels, mlp(): pl.pallas_call(mlp_kernel, out_shape=jax.ShapeDtypeStruct(hidden.shape, B...  67.9 us
    pallas_call x1, Pallas kernels, attention(): pl.pallas_call(attn_kernel, out_shape=(jax.ShapeDtypeStruct((n_rows, widt...  15.9 us
    unnamed x1, local copies, waits for them, and re-layouts  2.46 us

profile of v4, /device:TPU:1, one launch (start us, length us, event | category | flops | bytes accessed | tf_op | source)
XLA Modules:
  0.0 86.8 jit_solution(8894065785613075105)
XLA Ops:
  0.6 15.9 %attn.1 = (f32[256,1152]{1,0:T(8,128)}, bf16[64,512,128]{2,1,0:T(8,128)(2,1)}, bf16[64,512,128]{2,1,0:T(8,128)(2,1)}) custom-call(s32[64]{0:T(128)} %start_ref.1, bf16[256,2560]{1,0:T(8,128)(2,1)} %bitcast.12, f32[1,128]{1,0:T(1,128)} %constant.2.clone.freq_ref, bf16[20,128]{1,0:T(8,128)(2,1)} %bitcast.14, bf16[1,128]{1,0:T(2,128)(2,1)} %bitcast.16, ...), custom_call_target="tpu_custom_call" | custom-call | tf_op jit(solution)/shard_map/attn/pallas_call | solution.py:232
  16.5 67.9 %combine_mlp.1 = bf16[4,64,2560]{2,1,0:T(8,128)(2,1)} custom-call(f32[4,64,1152]{2,1,0:T(8,128)} %bitcast.13, bf16[4,64,2560]{2,1,0:T(8,128)(2,1)} %hid_ref.1, bf16[20,128]{1,0:T(8,128)(2,1)} %bitcast.15, bf16[1024,2560]{1,0:T(8,128)(2,1)} %wo_ref.1, bf16[2560,2432]{1,0:T(8,128)(2,1)} %wg_ref.1, bf16[2560,2432]{1,0:T(8,128)(2,1)} %wu_ref.1, ...), custom_call_target="tpu_custom_call" | custom-call | tf_op jit(solution)/shard_map/combine_mlp/pallas_call | solution.py:597
  84.4 2.5 %copy.20 = bf16[4,64,2560]{2,1,0:T(8,128)(2,1)} copy(bf16[4,64,2560]{2,1,0:T(8,128)(2,1)} %combine_mlp.1) | data formatting | bytes 2621440

commit v5 on v4

--- a/solution.py
+++ b/solution.py
@@ -17,8 +17,8 @@
 STATS = 128
 GROUP = 8
 PIECE = 256
-LAG = 4
-FLAG = 4
+LAG = 6
+FLAG = 8
 GU_BLOCK = 384
 PAIR = 2
 VMEM_LIMIT = 66_900_000
@@ -403,12 +403,12 @@
             return c
         lax.fori_loop(lo, hi, step, 0)
 
-    def parts(a, hf):
+    def parts(a, hf, sender=leaf):
         def body(i):
             for k in range(PAIR):
                 part(a, hf, i * PAIR + k)
 
-            @pl.when(leaf)
+            @pl.when(sender)
             def _():
                 for k in range(PAIR):
                     up(a, hf * n_pieces + i * PAIR + k).start()
@@ -480,8 +480,12 @@
 
     w_cps[0].wait()
     attn_half(0)
-    parts(0, 0)
+    parts(0, 0, jnp.logical_and(leaf, core == 0))
     attn_half(1)
+
+    @pl.when(jnp.logical_and(leaf, core == 1))
+    def _():
+        loop(0, n_pieces, lambda u: up(0, u).start())
     n_u = n_half * n_pieces
 
     @pl.when(leaf)

time: 87.1 us -> 84 us (0.964)
  Pallas kernels: 83.7 us -> 80.2 us
    pallas_call x1, Pallas kernels: 67.9 us -> 64.4 us  [mlp(): pl.pallas_call(mlp_kernel, out_shape=jax.ShapeDtypeStruct(hidden.shape, B...]
where the time goes in v5:
time: 84 us; the launch traced here: 83.3 us
  Pallas kernels  80.2 us (95%)
  local copies, waits for them, and re-layouts  2.46 us (3%)
    pallas_call x1, Pallas kernels, mlp(): pl.pallas_call(mlp_kernel, out_shape=jax.ShapeDtypeStruct(hidden.shape, B...  64.4 us
    pallas_call x1, Pallas kernels, attention(): pl.pallas_call(attn_kernel, out_shape=(jax.ShapeDtypeStruct((n_rows, widt...  15.9 us
    unnamed x1, local copies, waits for them, and re-layouts  2.46 us

profile of v5, /device:TPU:1, one launch (start us, length us, event | category | flops | bytes accessed | tf_op | source)
XLA Modules:
  0.0 83.3 jit_solution(3118964000877469645)
XLA Ops:
  0.6 15.9 %attn.1 = (f32[256,1152]{1,0:T(8,128)}, bf16[64,512,128]{2,1,0:T(8,128)(2,1)}, bf16[64,512,128]{2,1,0:T(8,128)(2,1)}) custom-call(s32[64]{0:T(128)} %start_ref.1, bf16[256,2560]{1,0:T(8,128)(2,1)} %bitcast.12, f32[1,128]{1,0:T(1,128)} %constant.2.clone.freq_ref, bf16[20,128]{1,0:T(8,128)(2,1)} %bitcast.14, bf16[1,128]{1,0:T(2,128)(2,1)} %bitcast.16, ...), custom_call_target="tpu_custom_call" | custom-call | tf_op jit(solution)/shard_map/attn/pallas_call | solution.py:232
  16.5 64.4 %combine_mlp.1 = bf16[4,64,2560]{2,1,0:T(8,128)(2,1)} custom-call(f32[4,64,1152]{2,1,0:T(8,128)} %bitcast.13, bf16[4,64,2560]{2,1,0:T(8,128)(2,1)} %hid_ref.1, bf16[20,128]{1,0:T(8,128)(2,1)} %bitcast.15, bf16[1024,2560]{1,0:T(8,128)(2,1)} %wo_ref.1, bf16[2560,2432]{1,0:T(8,128)(2,1)} %wg_ref.1, bf16[2560,2432]{1,0:T(8,128)(2,1)} %wu_ref.1, ...), custom_call_target="tpu_custom_call" | custom-call | tf_op jit(solution)/shard_map/combine_mlp/pallas_call | solution.py:601
  80.9 2.5 %copy.20 = bf16[4,64,2560]{2,1,0:T(8,128)(2,1)} copy(bf16[4,64,2560]{2,1,0:T(8,128)(2,1)} %combine_mlp.1) | data formatting | bytes 2621440

commit v6 on v5

--- a/solution.py
+++ b/solution.py
@@ -15,12 +15,12 @@
 BF16 = jnp.bfloat16
 MESH = pl.DeviceIdType.MESH
 STATS = 128
-GROUP = 8
-PIECE = 256
-LAG = 6
-FLAG = 8
+GROUP = 16
+PIECE = 512
+LAG = 3
+FLAG = 5
 GU_BLOCK = 384
-PAIR = 2
+PAIR = 1
 VMEM_LIMIT = 66_900_000
 
 

time: 84 us -> 83 us (0.988)
  Pallas kernels: 80.2 us -> 79.1 us
where the time goes in v6:
time: 83 us; the launch traced here: 82.2 us
  Pallas kernels  79.1 us (95%)
  local copies, waits for them, and re-layouts  2.46 us (3%)
    pallas_call x1, Pallas kernels, mlp(): pl.pallas_call(mlp_kernel, out_shape=jax.ShapeDtypeStruct(hidden.shape, B...  63.7 us
    pallas_call x1, Pallas kernels, attention(): pl.pallas_call(attn_kernel, out_shape=(jax.ShapeDtypeStruct((n_rows, widt...  15.4 us
    unnamed x1, local copies, waits for them, and re-layouts  2.46 us

profile of v6, /device:TPU:1, one launch (start us, length us, event | category | flops | bytes accessed | tf_op | source)
XLA Modules:
  0.0 82.2 jit_solution(8609141546222175692)
XLA Ops:
  0.6 15.4 %attn.1 = (f32[256,1152]{1,0:T(8,128)}, bf16[64,512,128]{2,1,0:T(8,128)(2,1)}, bf16[64,512,128]{2,1,0:T(8,128)(2,1)}) custom-call(s32[64]{0:T(128)} %start_ref.1, bf16[256,2560]{1,0:T(8,128)(2,1)} %bitcast.12, f32[1,128]{1,0:T(1,128)} %constant.2.clone.freq_ref, bf16[20,128]{1,0:T(8,128)(2,1)} %bitcast.14, bf16[1,128]{1,0:T(2,128)(2,1)} %bitcast.16, ...), custom_call_target="tpu_custom_call" | custom-call | tf_op jit(solution)/shard_map/attn/pallas_call | solution.py:232
  16.1 63.7 %combine_mlp.1 = bf16[4,64,2560]{2,1,0:T(8,128)(2,1)} custom-call(f32[4,64,1152]{2,1,0:T(8,128)} %bitcast.13, bf16[4,64,2560]{2,1,0:T(8,128)(2,1)} %hid_ref.1, bf16[20,128]{1,0:T(8,128)(2,1)} %bitcast.15, bf16[1024,2560]{1,0:T(8,128)(2,1)} %wo_ref.1, bf16[2560,2432]{1,0:T(8,128)(2,1)} %wg_ref.1, bf16[2560,2432]{1,0:T(8,128)(2,1)} %wu_ref.1, ...), custom_call_target="tpu_custom_call" | custom-call | tf_op jit(solution)/shard_map/combine_mlp/pallas_call | solution.py:601
  79.8 2.5 %copy.20 = bf16[4,64,2560]{2,1,0:T(8,128)(2,1)} copy(bf16[4,64,2560]{2,1,0:T(8,128)(2,1)} %combine_mlp.1) | data formatting | bytes 2621440
